TPU v7x, 8 devices: a whole 2x2x1 slice. The times are simulated.
8 devices in a mesh: rep: 1 (over z), dp: 8 (over x, y, core).
Axes of the slice: x: 2, y: 2, z: 1, core: 2. Of those that a mesh axis runs over, the one named last changes fastest.
Arguments:
- x: bfloat16 [8, 2048, 1024], P(('rep', 'dp'))
- dy: bfloat16 [8, 2048, 1024], P(('rep', 'dp'))
- w_gate: bfloat16 [2, 1024, 2560], P(None, 'dp')
- w_up: bfloat16 [2, 1024, 2560], P(None, 'dp')
- w_down: bfloat16 [2, 2560, 1024], P(None, 'dp')
Outputs:
- output 1: bfloat16 [8, 2048, 1024], P(('rep', 'dp'))
- output 2: bfloat16 [2, 1024, 2560], P('rep', 'dp')
- output 3: bfloat16 [2, 1024, 2560], P('rep', 'dp')
- output 4: bfloat16 [2, 2560, 1024], P('rep', 'dp')
All inputs are finite; a program needn't handle non-finite values.
Results may differ from a plain program's by a relative error of at most 0.018.
Values are sent between devices in bfloat16 or wider.
A program may use at most 2 GiB of HBM per device.

v0:
```python
import jax
import jax.numpy as jnp
from jax import lax

NAMES = ("w_gate", "w_up", "w_down")


def matmul(a, w):
    return jnp.dot(a, w, preferred_element_type=jnp.float32).astype(jnp.bfloat16)


def normed(h):
    wide = h.astype(jnp.float32)
    scale = lax.rsqrt(jnp.mean(wide**2, -1, keepdims=True) + 1e-6)
    return (wide * scale).astype(jnp.bfloat16)


def layer(h, w):
    a = normed(h)
    gate = jnp.dot(a, w["w_gate"], preferred_element_type=jnp.float32)
    up = jnp.dot(a, w["w_up"], preferred_element_type=jnp.float32)
    return h + matmul((jax.nn.silu(gate) * up).astype(jnp.bfloat16), w["w_down"])


def stack(weights, h):
    for number in range(weights["w_gate"].shape[0]):
        h = layer(h, {name: w[number] for name, w in weights.items()})
    return h


def solution(mesh):
    groups = mesh.shape["rep"]

    def step(x, dy, *weights):
        shape = x.shape
        x, dy = (t.reshape(groups, -1, *t.shape[1:]) for t in (x, dy))

        def of_a_group(x, dy):
            _, back = jax.vjp(stack, dict(zip(NAMES, weights, strict=True)), x)
            by_weights, by_x = back(dy)
            return (by_x, *(by_weights[name] for name in NAMES))

        by_x, *by_weights = jax.vmap(of_a_group)(x, dy)
        return (by_x.reshape(shape), *(t.reshape(-1, *t.shape[2:]) for t in by_weights))

    return step
```

profile of v0, /device:TPU:0, one launch (start us, length us, event | category | flops | bytes accessed | tf_op | source)
XLA Modules:
  0.0 745.5 jit_solution(449238131105903546)
XLA Ops:
  7.2 2.4 fusion.91
  9.7 0.0 all-gather.32.cloned.1.call-start
  9.7 2.4 fusion.90
  12.2 0.0 all-gather.34.cloned.1.call-start
  12.2 2.4 fusion.92
  14.7 0.0 all-gather.38.cloned.1.call-start
  14.7 0.5 all-gather.38.cloned.1.call-update
  15.3 0.5 all-gather.36.cloned.1.call-update
  15.9 0.5 all-gather.40.cloned.1.call-update
  16.5 6.5 copy.1
  23.0 3.1 fusion.36
  26.1 0.6 copy-done.9
  26.7 6.4 copy.2
  33.1 14.7 %all-gather.30.cloned.1.call-done = bf16[1,1024,2560]{2,1,0:T(8,128)(2,1)} async-done(((bf16[1,128,2560]{2,1,0:T(8,128)(2,1)}), bf16[1,1024,2560]{2,1,0:T(8,128)(2,1)}) %all-gather.30.cloned.1.call-update) | async-done | bytes 5242896 | tf_op jit(solution)/vmap(jvp())/squeeze | solution.py:27
  47.8 18.3 %fusion.58 = f32[2048,2560]{1,0:T(8,128)} fusion(bf16[1,1024,2560]{2,1,0:T(8,128)(2,1)} %all-gather.30.cloned.1.call-done, bf16[1,2048,1024]{1,2,0:T(8,128)(2,1)} %copy.1, f32[2048]{0:T(1024)S(1)} %bitcast.243), kind=kOutput, calls=%fused_computation.79 | convolution fusion | flops 10743709696 | bytes 30416896 | tf_op jit(solution)/vmap(jvp())/dot_general | solution.py:20
  66.1 19.2 %all-gather.32.cloned.1.call-done = bf16[1,1024,2560]{2,1,0:T(8,128)(2,1)} async-done(((bf16[1,128,2560]{2,1,0:T(8,128)(2,1)}), bf16[1,1024,2560]{2,1,0:T(8,128)(2,1)}) %all-gather.32.cloned.1.call-update) | async-done | bytes 5242896 | tf_op jit(solution)/vmap(jvp())/squeeze | solution.py:27
  85.4 19.0 %fusion.54 = f32[2048,2560]{1,0:T(8,128)} fusion(bf16[1,1024,2560]{2,1,0:T(8,128)(2,1)} %all-gather.32.cloned.1.call-done, bf16[1,2048,1024]{1,2,0:T(8,128)(2,1)} %copy.1, f32[2048]{0:T(1024)S(1)} %bitcast.244), kind=kOutput, calls=%fused_computation.75 | convolution fusion | flops 10743709696 | bytes 30416896 | tf_op jit(solution)/vmap(jvp())/dot_general | solution.py:21
  104.4 15.3 %fusion.24 = bf16[2048,2560]{1,0:T(8,128)(2,1)} fusion(f32[2048,2560]{1,0:T(8,128)} %fusion.54, f32[2048,2560]{1,0:T(8,128)S(1)} %copy-done), kind=kLoop, calls=%fused_computation.46 | loop fusion | flops 31457280 | bytes 52428800
  119.6 2.7 all-gather.34.cloned.1.call-done
  122.4 18.0 %fusion.39 = (f32[2048]{0:T(1024)S(1)}, bf16[1,2048,1024]{1,2,0:T(8,128)(2,1)}) fusion(bf16[1,2048,1024]{1,2,0:T(8,128)(2,1)} %copy.1, bf16[2048,2560]{1,0:T(8,128)(2,1)} %fusion.24, bf16[1,2560,1024]{2,1,0:T(8,128)(2,1)} %all-gather.34.cloned.1.call-done), kind=kOutput, calls=%fused_computation.60 | convolution fusion | flops 10747901952 | bytes 24125440 | tf_op jit(solution)/vmap(jvp())/dot_general | solution.py:9
  140.4 0.6 copy-done.11
  141.0 18.2 %all-gather.38.cloned.1.call-done = bf16[1,2560,1024]{2,1,0:T(8,128)(2,1)} async-done(((bf16[1,320,1024]{2,1,0:T(8,128)(2,1)}), bf16[1,2560,1024]{2,1,0:T(8,128)(2,1)}) %all-gather.38.cloned.1.call-update) | async-done | bytes 5242896 | tf_op jit(solution)/vmap(jvp())/squeeze | solution.py:27
  159.2 16.8 %convolution_convert_fusion.1 = bf16[2048,2560]{1,0:T(8,128)(2,1)} fusion(bf16[1,2560,1024]{2,1,0:T(8,128)(2,1)} %all-gather.38.cloned.1.call-done, bf16[1,2048,1024]{2,1,0:T(8,128)(2,1)} %param), kind=kOutput, calls=%fused_computation.43 | convolution fusion | flops 10742661120 | bytes 19922944 | tf_op jit(solution)/vmap(transpose(jvp()))/dot_general | solution.py:9
  176.0 20.6 %all-gather.36.cloned.1.call-done = bf16[1,1024,2560]{2,1,0:T(8,128)(2,1)} async-done(((bf16[1,128,2560]{2,1,0:T(8,128)(2,1)}), bf16[1,1024,2560]{2,1,0:T(8,128)(2,1)}) %all-gather.36.cloned.1.call-update) | async-done | bytes 5242896 | tf_op jit(solution)/vmap(jvp())/squeeze | solution.py:27
  196.6 18.5 %fusion.48 = f32[2048,2560]{1,0:T(8,128)} fusion(bf16[1,1024,2560]{2,1,0:T(8,128)(2,1)} %all-gather.36.cloned.1.call-done, bf16[1,2048,1024]{1,2,0:T(8,128)(2,1)} %get-tuple-element.11, f32[2048]{0:T(1024)S(1)} %bitcast.248), kind=kOutput, calls=%fused_computation.69 | convolution fusion | flops 10743709696 | bytes 30416896 | tf_op jit(solution)/vmap(jvp())/dot_general | solution.py:20
  215.1 22.5 %fusion.20 = f32[2560,1024]{1,0:T(8,128)} fusion(bf16[2048,2560]{1,0:T(8,128)(2,1)} %convolution_convert_fusion.1, f32[2048,2560]{1,0:T(8,128)} %fusion.48, bf16[1,2048,1024]{1,2,0:T(8,128)(2,1)} %get-tuple-element.11, f32[2048]{0:T(1024)S(1)} %bitcast.249), kind=kOutput, calls=%fused_computation.40 | convolution fusion | flops 10775166976 | bytes 46145536 | tf_op jit(solution)/vmap(transpose(jvp()))/dot_general | solution.py:21
  237.7 0.0 reduce-scatter.25.cloned.1.call-start
  237.7 18.7 %fusion.42 = f32[2048,2560]{1,0:T(8,128)} fusion(bf16[1,1024,2560]{2,1,0:T(8,128)(2,1)} %all-gather.40.cloned.1.call-done, bf16[1,2048,1024]{1,2,0:T(8,128)(2,1)} %get-tuple-element.11, f32[2048]{0:T(1024)S(1)} %bitcast.250), kind=kOutput, calls=%fused_computation.63 | convolution fusion | flops 10743709696 | bytes 30416896 | tf_op jit(solution)/vmap(jvp())/dot_general | solution.py:21
  256.5 19.8 %fusion.22 = bf16[2048,1024]{0,1:T(8,128)(2,1)} fusion(bf16[2048,2560]{1,0:T(8,128)(2,1)} %convolution_convert_fusion.1, f32[2048,2560]{1,0:T(8,128)} %fusion.48, bf16[1,1024,2560]{2,1,0:T(8,128)(2,1)} %all-gather.40.cloned.1.call-done), kind=kOutput, calls=%fused_computation.41 | convolution fusion | flops 10768875520 | bytes 40894464 | tf_op jit(solution)/vmap(transpose(jvp()))/dot_general | solution.py:21
  276.3 18.5 %fusion.4 = bf16[2048,2560]{1,0:T(8,128)(2,1)S(1)} fusion(f32[2048,2560]{1,0:T(8,128)} %fusion.48, f32[2048,2560]{1,0:T(8,128)} %fusion.42, bf16[2048,2560]{1,0:T(8,128)(2,1)} %convolution_convert_fusion.1), kind=kLoop, calls=%fused_computation.10 | loop fusion | flops 62914560 | bytes 62914560
  294.8 19.1 %fusion.41 = (f32[2048]{0:T(1024)S(1)}, bf16[2048,1024]{0,1:T(8,128)(2,1)}) fusion(bf16[1,2048,1024]{1,2,0:T(8,128)(2,1)S(1)} %copy-done.8, bf16[2048,1024]{0,1:T(8,128)(2,1)} %fusion.22, bf16[2048,2560]{1,0:T(8,128)(2,1)S(1)} %fusion.4, bf16[1,1024,2560]{2,1,0:T(8,128)(2,1)} %all-gather.36.cloned.1.call-done), kind=kOutput, calls=%fused_computation.62 | convolution fusion | flops 10747901952 | bytes 28319744 | tf_op jit(solution)/vmap(transpose(jvp()))/dot_general | solution.py:20
  313.9 5.4 fusion.63
  319.4 2.0 copy-done.3
  321.4 15.8 %convolution_convert_fusion = bf16[2048,2560]{1,0:T(8,128)(2,1)} fusion(bf16[1,2560,1024]{2,1,0:T(8,128)(2,1)} %all-gather.34.cloned.1.call-done, bf16[1,2048,1024]{1,2,0:T(8,128)(2,1)S(1)} %fusion.63), kind=kOutput, calls=%fused_computation.42 | convolution fusion | flops 10742661120 | bytes 19922944 | tf_op jit(solution)/vmap(transpose(jvp()))/dot_general | solution.py:9
  337.2 22.8 %fusion.16 = f32[2560,1024]{1,0:T(8,128)} fusion(bf16[2048,2560]{1,0:T(8,128)(2,1)} %convolution_convert_fusion, f32[2048,2560]{1,0:T(8,128)} %fusion.58, bf16[1,2048,1024]{1,2,0:T(8,128)(2,1)} %copy.1, f32[2048]{0:T(1024)S(1)} %bitcast.245), kind=kOutput, calls=%fused_computation.38 | convolution fusion | flops 10775166976 | bytes 46145536 | tf_op jit(solution)/vmap(transpose(jvp()))/dot_general | solution.py:21
  360.0 0.0 reduce-scatter.19.cloned.1.call-start
  360.0 17.7 %fusion.81 = f32[2560,1024]{1,0:T(8,128)} fusion(bf16[2048,2560]{1,0:T(8,128)(2,1)} %copy-done.7, bf16[1,2048,1024]{1,2,0:T(8,128)(2,1)} %get-tuple-element.11, f32[2048]{0:T(1024)S(1)} %bitcast.252), kind=kOutput, calls=%fused_computation.94 | convolution fusion | flops 10743709696 | bytes 25174016 | tf_op jit(solution)/vmap(transpose(jvp()))/dot_general | solution.py:20
  377.8 0.0 reduce-scatter.21.cloned.1.call-start
  377.9 18.6 %fusion.7 = bf16[2048,2560]{1,0:T(8,128)(2,1)S(1)} fusion(f32[2048,2560]{1,0:T(8,128)} %fusion.58, f32[2048,2560]{1,0:T(8,128)} %fusion.54, bf16[2048,2560]{1,0:T(8,128)(2,1)} %convolution_convert_fusion), kind=kLoop, calls=%fused_computation.13 | loop fusion | flops 62914560 | bytes 62914560
  396.5 3.9 copy-done.6
  400.4 13.7 %fusion.76 = f32[2560,1024]{1,0:T(8,128)} fusion(bf16[2048,2560]{1,0:T(8,128)(2,1)S(1)} %fusion.7, bf16[1,2048,1024]{1,2,0:T(8,128)(2,1)S(1)} %copy-done.1, f32[2048]{0:T(1024)S(1)} %bitcast.246), kind=kOutput, calls=%fused_computation.93 | convolution fusion | flops 10743709696 | bytes 25174016 | tf_op jit(solution)/vmap(transpose(jvp()))/dot_general | solution.py:20
  414.1 0.0 reduce-scatter.27.cloned.1.call-start
  414.2 23.0 %fusion.26 = f32[2560,1024]{1,0:T(8,128)} fusion(f32[2048,2560]{1,0:T(8,128)} %fusion.42, f32[2048,2560]{1,0:T(8,128)} %fusion.48, bf16[1,2048,1024]{2,1,0:T(8,128)(2,1)} %param), kind=kOutput, calls=%fused_computation.48 | convolution fusion | flops 10768875520 | bytes 56623104 | tf_op jit(solution)/vmap(transpose(jvp()))/dot_general | solution.py:9
  437.3 0.0 reduce-scatter.29.cloned.1.call-start
  437.3 17.5 %fusion.64 = f32[1024,2560]{0,1:T(8,128)} fusion(bf16[2048,2560]{1,0:T(8,128)(2,1)} %fusion.24, bf16[1,2048,1024]{1,2,0:T(8,128)(2,1)} %copy-done.3), kind=kOutput, calls=%fused_computation.85 | convolution fusion | flops 10737418240 | bytes 25165824 | tf_op jit(solution)/vmap(transpose(jvp()))/dot_general | solution.py:9
  454.9 19.8 %fusion.18 = bf16[2048,1024]{0,1:T(8,128)(2,1)} fusion(bf16[2048,2560]{1,0:T(8,128)(2,1)} %convolution_convert_fusion, f32[2048,2560]{1,0:T(8,128)} %fusion.58, bf16[1,1024,2560]{2,1,0:T(8,128)(2,1)} %all-gather.32.cloned.1.call-done), kind=kOutput, calls=%fused_computation.39 | convolution fusion | flops 10768875520 | bytes 40894464 | tf_op jit(solution)/vmap(transpose(jvp()))/dot_general | solution.py:21
  474.7 17.7 %fusion.38 = (f32[2048]{0:T(1024)S(1)}, bf16[2048,1024]{0,1:T(8,128)(2,1)S(1)}) fusion(bf16[1,2048,1024]{1,2,0:T(8,128)(2,1)} %copy.1, bf16[2048,1024]{0,1:T(8,128)(2,1)} %fusion.18, bf16[2048,2560]{1,0:T(8,128)(2,1)} %copy-done.6, bf16[1,1024,2560]{2,1,0:T(8,128)(2,1)} %all-gather.30.cloned.1.call-done), kind=kOutput, calls=%fused_computation.59 | convolution fusion | flops 10747901952 | bytes 28319744 | tf_op jit(solution)/vmap(transpose(jvp()))/dot_general | solution.py:20
  492.5 4.7 fusion.62
  497.2 6.4 copy.3
  503.6 1.4 convert_bitcast_fusion.3
  505.0 1.4 convert_bitcast_fusion.2
  506.4 0.1 add_bitcast_fusion.1
  506.5 1.4 copy.5
  507.9 0.6 reduce-scatter.19.cloned.1.call-done
  508.5 1.4 convert_bitcast_fusion.5
  509.9 74.4 %reduce-scatter.21.cloned.1.call-done = f32[2560,128]{1,0:T(8,128)} async-done(((f32[2560,1024]{1,0:T(8,128)}), f32[2560,128]{1,0:T(8,128)}) %reduce-scatter.21.cloned.1.call-update) | async-done | bytes 1310736
  584.2 1.4 convert_bitcast_fusion.4
  585.6 0.1 add_bitcast_fusion.2
  585.7 1.4 copy.4
  587.2 73.0 %reduce-scatter.27.cloned.1.call-done = f32[320,1024]{1,0:T(8,128)} async-done(((f32[2560,1024]{1,0:T(8,128)}), f32[320,1024]{1,0:T(8,128)}) %reduce-scatter.27.cloned.1.call-update) | async-done | bytes 1310736
  660.1 1.4 convert_bitcast_fusion.1
  661.5 74.3 %reduce-scatter.29.cloned.1.call-done = f32[1024,320]{0,1:T(8,128)} async-done(((f32[1024,2560]{0,1:T(8,128)}), f32[1024,320]{0,1:T(8,128)}) %reduce-scatter.29.cloned.1.call-update) | async-done | bytes 1310736
  735.9 1.4 convert_bitcast_fusion
  737.3 1.1 add_bitcast_fusion
  (50 shorter events, 0.5 us)
Async XLA Ops:
  7.2 40.6 %all-gather.30.cloned.1.call-start = ((), (), s32[]{:S(2)}) async-start(), calls=%async_computation.6 | async-start | bytes 5898240 | tf_op jit(solution)/vmap(jvp())/squeeze | solution.py:27
  9.7 75.7 %all-gather.32.cloned.1.call-start = ((), (), s32[]{:S(2)}) async-start(), calls=%async_computation.7 | async-start | bytes 5898240 | tf_op jit(solution)/vmap(jvp())/squeeze | solution.py:27
  12.2 110.2 %all-gather.34.cloned.1.call-start = ((), (), s32[]{:S(2)}) async-start(), calls=%async_computation.8 | async-start | bytes 5898240 | tf_op jit(solution)/vmap(jvp())/squeeze | solution.py:27
  14.7 144.5 %all-gather.38.cloned.1.call-start = ((), (), s32[]{:S(2)}) async-start(), calls=%async_computation.10 | async-start | bytes 5898240 | tf_op jit(solution)/vmap(jvp())/squeeze | solution.py:27
  15.3 181.4 %all-gather.36.cloned.1.call-start = ((), (), s32[]{:S(2)}) async-start(), calls=%async_computation.9 | async-start | bytes 5898240 | tf_op jit(solution)/vmap(jvp())/squeeze | solution.py:27
  15.9 221.9 %all-gather.40.cloned.1.call-start = ((), (), s32[]{:S(2)}) async-start(), calls=%async_computation.11 | async-start | bytes 5898240 | tf_op jit(solution)/vmap(jvp())/squeeze | solution.py:27
  16.4 487.1 %reduce-scatter.23.cloned.1.call-start = ((), (), s32[]{:S(2)}) async-start(), calls=%async_computation.14 | async-start | bytes 11796480
  26.1 0.6 copy-start.9
  26.7 58.7 %copy-start.13 = (f32[1,2048]{1,0:T(1,128)}, f32[1,2048]{1,0:T(1,128)S(1)}, u32[]{:S(2)}) copy-start(f32[1,2048]{1,0:T(1,128)S(1)} %rsqrt.22) | copy-start | bytes 24580
  85.4 19.0 %copy-start = (f32[2048,2560]{1,0:T(8,128)S(1)}, f32[2048,2560]{1,0:T(8,128)}, u32[]{:S(2)}) copy-start(f32[2048,2560]{1,0:T(8,128)} %fusion.58) | copy-start | bytes 62914564
  140.4 0.6 copy-start.11
  237.7 267.3 %reduce-scatter.25.cloned.1.call-start = ((), (), s32[]{:S(2)}) async-start(), calls=%async_computation.15 | async-start | bytes 11796480
  276.3 18.5 %copy-start.8 = (bf16[1,2048,1024]{1,2,0:T(8,128)(2,1)S(1)}, bf16[1,2048,1024]{1,2,0:T(8,128)(2,1)}, u32[]{:S(2)}) copy-start(bf16[1,2048,1024]{1,2,0:T(8,128)(2,1)} %get-tuple-element.11) | copy-start | bytes 12582916
  294.8 19.1 %copy-start.7 = (bf16[2048,2560]{1,0:T(8,128)(2,1)}, bf16[2048,2560]{1,0:T(8,128)(2,1)S(1)}, u32[]{:S(2)}) copy-start(bf16[2048,2560]{1,0:T(8,128)(2,1)S(1)} %fusion.4) | copy-start | bytes 31457284
  294.8 19.1 %copy-start.12 = (f32[2048]{0:T(1024)S(1)}, f32[2048]{0:T(1024)}, u32[]{:S(2)}) copy-start(f32[2048]{0:T(1024)} %copy-done.11) | copy-start | bytes 24580
  294.8 19.1 %copy-start.5 = (bf16[1,2048,1024]{1,2,0:T(8,128)(2,1)S(1)}, bf16[1,2048,1024]{1,2,0:T(8,128)(2,1)}, u32[]{:S(2)}) copy-start(bf16[1,2048,1024]{1,2,0:T(8,128)(2,1)} %copy.2) | copy-start | bytes 12582916
  319.4 2.0 copy-start.3
  321.4 15.8 %copy-start.14 = (f32[1,2048]{1,0:T(1,128)S(1)}, f32[1,2048]{1,0:T(1,128)}, u32[]{:S(2)}) copy-start(f32[1,2048]{1,0:T(1,128)} %copy-done.13) | copy-start | bytes 24580
  360.0 148.5 %reduce-scatter.19.cloned.1.call-start = ((), (), s32[]{:S(2)}) async-start(), calls=%async_computation.12 | async-start | bytes 11796480
  377.8 206.4 %reduce-scatter.21.cloned.1.call-start = ((), (), s32[]{:S(2)}) async-start(), calls=%async_computation.13 | async-start | bytes 11796480
  377.9 22.5 %copy-start.1 = (bf16[1,2048,1024]{1,2,0:T(8,128)(2,1)S(1)}, bf16[1,2048,1024]{1,2,0:T(8,128)(2,1)}, u32[]{:S(2)}) copy-start(bf16[1,2048,1024]{1,2,0:T(8,128)(2,1)} %copy.1) | copy-start | bytes 12582916
  396.5 3.9 copy-start.6
  414.1 246.0 %reduce-scatter.27.cloned.1.call-start = ((), (), s32[]{:S(2)}) async-start(), calls=%async_computation.16 | async-start | bytes 11796480
  437.3 298.6 %reduce-scatter.29.cloned.1.call-start = ((), (), s32[]{:S(2)}) async-start(), calls=%async_computation.17 | async-start | bytes 11796480
  474.7 17.8 %copy-start.10 = (f32[2048]{0:T(1024)S(1)}, f32[2048]{0:T(1024)}, u32[]{:S(2)}) copy-start(f32[2048]{0:T(1024)} %copy-done.9) | copy-start | bytes 24580
  474.7 17.8 %copy-start.2 = (bf16[1,2048,1024]{1,2,0:T(8,128)(2,1)S(1)}, bf16[1,2048,1024]{1,2,0:T(8,128)(2,1)}, u32[]{:S(2)}) copy-start(bf16[1,2048,1024]{1,2,0:T(8,128)(2,1)} %copy.1) | copy-start | bytes 12582916
  474.7 17.8 %copy-start.4 = (bf16[1,2048,1024]{1,2,0:T(8,128)(2,1)S(1)}, bf16[1,2048,1024]{1,2,0:T(8,128)(2,1)}, u32[]{:S(2)}) copy-start(bf16[1,2048,1024]{1,2,0:T(8,128)(2,1)} %copy-done.3) | copy-start | bytes 12582916
  474.7 17.8 %copy-start.15 = (f32[1,2048]{1,0:T(1,128)S(1)}, f32[1,2048]{1,0:T(1,128)}, u32[]{:S(2)}) copy-start(f32[1,2048]{1,0:T(1,128)} %copy-done.13) | copy-start | bytes 24580
Sparse Core Ops, SparseCore 0:
  9.8 37.9 all-gather.29
  50.2 35.1 all-gather.31
  87.2 35.1 all-gather.33
  124.0 35.1 all-gather.37
  161.4 35.1 all-gather.35
  198.9 35.1 all-gather.39
  237.8 72.4 reduce-scatter.22
  360.1 72.4 reduce-scatter.24
  436.0 72.4 reduce-scatter.18
  511.8 72.4 reduce-scatter.20
  587.7 72.4 reduce-scatter.26
  663.4 72.4 reduce-scatter.28
where the time goes:
time: 752 us; the launch traced here: 746 us
  matrix products  319 us (42%)
  waiting for transfers between devices  299 us (40%)
  other arithmetic  75.2 us (10%)
  local copies, waits for them, and re-layouts  36.7 us (5%)
  between operations  14.7 us (2%)
    unnamed x18, waiting for transfers between devices  224 us
    dot_general x6, matrix products, layer(): up = jnp.dot(a, w['w_up'], preferred_element_type=jnp.float32)  123 us
    dot_general x6, matrix products, layer(): gate = jnp.dot(a, w['w_gate'], preferred_element_type=jnp.float32)  105 us
    dot_general x5, matrix products, matmul(): jnp.dot(a, w, preferred_element_type=jnp.float32).astype(jnp.bfloat16)  91.2 us
    squeeze x6, waiting for transfers between devices, stack(): h = layer(h, {name: w[number] for name, w in weights.items()})  75.5 us
    unnamed x3, other arithmetic  52.3 us
    unnamed x37, local copies, waits for them, and re-layouts  29.3 us
  transfers between devices with their start and end apart: 12, of which 9 were waited for; matrix products, arithmetic and copies ran while one was open for 56% of the time, Pallas kernels for 0%

commit v1 on v0

v1 whole, which is shorter than its diff:
```python
import jax
import jax.numpy as jnp
from jax import lax
from jax.sharding import PartitionSpec as P

F32, BF16 = jnp.float32, jnp.bfloat16


def dot(a, b, dims):
    return lax.dot_general(a, b, (dims, ((), ())), preferred_element_type=F32)


def norm(h):
    wide = h.astype(F32)
    scale = lax.rsqrt(jnp.mean(wide**2, -1, keepdims=True) + 1e-6)
    return wide, scale, (wide * scale).astype(BF16)


def solution(mesh):
    def gather(w):
        return lax.all_gather(w, "dp", axis=0, tiled=True)

    def scatter(g):
        return lax.psum_scatter(g.astype(BF16), "dp", scatter_dimension=0, tiled=True)

    def body(x, dy, wg, wu, wd):
        layers = wg.shape[0]
        h, dh = x[0], dy[0]
        weights = [tuple(gather(w[n]) for w in (wg, wu, wd)) for n in range(layers)]
        saved = []
        for n in range(layers):
            g_w, u_w, d_w = weights[n]
            wide, scale, a = norm(h)
            gate = dot(a, g_w, ((1,), (0,)))
            up = dot(a, u_w, ((1,), (0,)))
            p = (jax.nn.silu(gate) * up).astype(BF16)
            saved.append((wide, scale, a, gate, up, p))
            if n + 1 < layers:
                h = h + dot(p, d_w, ((1,), (0,))).astype(BF16)
        grads = [None] * layers
        for n in reversed(range(layers)):
            g_w, u_w, d_w = weights[n]
            wide, scale, a, gate, up, p = saved[n]
            dp = dot(dh, d_w, ((1,), (1,))).astype(BF16).astype(F32)
            by_d = scatter(dot(p, dh, ((0,), (0,))))
            sig = jax.nn.sigmoid(gate)
            d_gate = (dp * up * (sig * (1 + gate * (1 - sig)))).astype(BF16)
            d_up = (dp * (gate * sig)).astype(BF16)
            by_g = scatter(dot(a, d_gate, ((0,), (0,))))
            by_u = scatter(dot(a, d_up, ((0,), (0,))))
            da = dot(d_gate, g_w, ((1,), (1,))) + dot(d_up, u_w, ((1,), (1,)))
            da = da.astype(BF16).astype(F32)
            inner = jnp.mean(da * wide, -1, keepdims=True)
            back = scale * da - wide * (scale**3 * inner)
            dh = dh + back.astype(BF16)
            grads[n] = (by_g, by_u, by_d)
        return (dh[None], *(jnp.stack([g[i] for g in grads]) for i in range(3)))

    act = P(("rep", "dp"), None, None)
    w = P(None, "dp", None)
    return jax.shard_map(
        body, mesh=mesh, in_specs=(act, act, w, w, w), out_specs=(act, *[P("rep", "dp", None)] * 3), check_vma=False
    )
```

time: 752 us -> 640 us (0.85)
  waiting for transfers between devices: 299 us -> 234 us
  other arithmetic: 75.2 us -> 18.8 us
  matrix products: 319 us -> 337 us
    unnamed x18 -> x12, waiting for transfers between devices: 224 us -> 1.73 us
    reduce_scatter x0 -> x6, waiting for transfers between devices: none -> 133 us  [scatter(): lax.psum_scatter(g.astype(BF16), 'dp', scatter_dimension=0, tiled=True)]
    all_gather x0 -> x6, waiting for transfers between devices: none -> 99 us  [gather(): return lax.all_gather(w, 'dp', axis=0, tiled=True)]
    squeeze x6 -> x0, waiting for transfers between devices: 75.5 us -> none  [stack(): h = layer(h, {name: w[number] for name, w in weights.items()})]
    unnamed x3 -> x0, other arithmetic: 52.3 us -> none
    dot_general x17, matrix products: 319 us -> 337 us  [dot(): return lax.dot_general(a, b, (dims, ((), ())), preferred_element_type=F32)]
    add_any x2 -> x0, other arithmetic: 10.1 us -> none  [normed(): wide = h.astype(jnp.float32)]
    unnamed x37 -> x23, local copies, waits for them, and re-layouts: 29.3 us -> 22 us
  transfers between devices with their start and end apart: 12 -> 12, of which waited for: 9 -> 9; matrix products, arithmetic and copies ran while one was open for 56% -> 46% of each run, Pallas kernels for 0% -> 0%
where the time goes in v1:
time: 640 us; the launch traced here: 634 us
  matrix products  337 us (53%)
  waiting for transfers between devices  234 us (37%)
  local copies, waits for them, and re-layouts  29.3 us (5%)
  other arithmetic  18.8 us (3%)
  between operations  14.8 us (2%)
    dot_general x17, matrix products, dot(): return lax.dot_general(a, b, (dims, ((), ())), preferred_element_type=F32)  337 us
    reduce_scatter x6, waiting for transfers between devices, scatter(): lax.psum_scatter(g.astype(BF16), 'dp', scatter_dimension=0, tiled=True)  133 us
    all_gather x6, waiting for transfers between devices, gather(): return lax.all_gather(w, 'dp', axis=0, tiled=True)  99 us
    unnamed x23, local copies, waits for them, and re-layouts  22 us
  transfers between devices with their start and end apart: 12, of which 9 were waited for; matrix products, arithmetic and copies ran while one was open for 46% of the time, Pallas kernels for 0%

profile of v1, /device:TPU:0, one launch (start us, length us, event | category | flops | bytes accessed | tf_op | source)
XLA Modules:
  0.0 633.9 jit_solution(11583664888438881808)
XLA Ops:
  7.2 0.0 all-gather.13.cloned.1.call-start
  7.2 2.4 fusion.63
  9.6 0.0 all-gather.13.cloned.1.call-update
  9.7 0.0 all-gather.15.cloned.1.call-start
  9.7 2.4 fusion.65
  12.2 0.0 all-gather.15.cloned.1.call-update
  12.2 0.0 all-gather.17.cloned.1.call-start
  12.2 2.4 fusion.64
  14.7 0.0 all-gather.17.cloned.1.call-update
  14.7 0.0 all-gather.21.cloned.1.call-start
  14.8 0.5 all-gather.21.cloned.1.call-update
  15.3 0.0 all-gather.23.cloned.1.call-start
  15.3 0.5 all-gather.23.cloned.1.call-update
  15.9 0.0 all-gather.19.cloned.1.call-start
  15.9 0.5 all-gather.19.cloned.1.call-update
  16.4 0.0 reduce-scatter.15.cloned.1.call-start
  16.5 6.4 %copy.10 = bf16[1,2048,1024]{1,2,0:T(8,128)(2,1)} copy(bf16[1,2048,1024]{2,1,0:T(8,128)(2,1)} %param.5) | data formatting | bytes 8388608 | tf_op args[0]
  22.9 3.1 fusion.13
  26.0 0.6 copy-done.6
  26.6 6.5 %copy.9 = bf16[1,2048,1024]{1,2,0:T(8,128)(2,1)} copy(bf16[1,2048,1024]{2,1,0:T(8,128)(2,1)} %param.6) | data formatting | bytes 8388608 | tf_op args[1]
  33.1 15.3 %all-gather.13.cloned.1.call-done = bf16[1,1024,2560]{2,1,0:T(8,128)(2,1)} async-done(((bf16[1,128,2560]{2,1,0:T(8,128)(2,1)}), bf16[1,1024,2560]{2,1,0:T(8,128)(2,1)}) %all-gather.13.cloned.1.call-update) | async-done | bytes 5242896 | tf_op jit(solution)/shard_map/all_gather | solution.py:21
  48.4 18.4 %fusion.38 = f32[2048,2560]{1,0:T(8,128)} fusion(bf16[1,1024,2560]{2,1,0:T(8,128)(2,1)} %all-gather.13.cloned.1.call-done, bf16[1,2048,1024]{1,2,0:T(8,128)(2,1)} %copy.10, f32[2048]{0:T(1024)S(1)} %add_rsqrt_fusion.1), kind=kOutput, calls=%fused_computation.65 | convolution fusion | flops 10743709696 | bytes 30416896 | tf_op jit(solution)/shard_map/dot_general | solution.py:10
  66.7 18.6 %all-gather.15.cloned.1.call-done = bf16[1,1024,2560]{2,1,0:T(8,128)(2,1)} async-done(((bf16[1,128,2560]{2,1,0:T(8,128)(2,1)}), bf16[1,1024,2560]{2,1,0:T(8,128)(2,1)}) %all-gather.15.cloned.1.call-update) | async-done | bytes 5242896 | tf_op jit(solution)/shard_map/all_gather | solution.py:21
  85.4 28.9 %multiply_convert_fusion.1 = (bf16[2048,2560]{1,0:T(8,128)(2,1)}, f32[2048,2560]{1,0:T(8,128)}) fusion(f32[2048,2560]{1,0:T(8,128)} %fusion.38, bf16[1,1024,2560]{2,1,0:T(8,128)(2,1)} %all-gather.15.cloned.1.call-done, bf16[1,2048,1024]{1,2,0:T(8,128)(2,1)} %copy.10, f32[2048]{0:T(1024)S(1)} %add_rsqrt_fusion.1), kind=kOutput, calls=%fused_computation.13 | convolution fusion | flops 10775166976 | bytes 61874176 | tf_op jit(solution)/shard_map/dot_general | solution.py:10
  114.3 8.1 %all-gather.17.cloned.1.call-done = bf16[1,2560,1024]{2,1,0:T(8,128)(2,1)} async-done(((bf16[1,320,1024]{2,1,0:T(8,128)(2,1)}), bf16[1,2560,1024]{2,1,0:T(8,128)(2,1)}) %all-gather.17.cloned.1.call-update) | async-done | bytes 5242896 | tf_op jit(solution)/shard_map/all_gather | solution.py:21
  122.4 17.9 %fusion.16 = (f32[2048]{0:T(1024)S(1)}, bf16[2048,1024]{0,1:T(8,128)(2,1)}) fusion(bf16[2048,2560]{1,0:T(8,128)(2,1)} %get-tuple-element.18, bf16[1,2560,1024]{2,1,0:T(8,128)(2,1)} %all-gather.17.cloned.1.call-done, bf16[1,2048,1024]{1,2,0:T(8,128)(2,1)} %copy.10), kind=kOutput, calls=%fused_computation.36 | convolution fusion | flops 10747901952 | bytes 24125440 | tf_op jit(solution)/shard_map/dot_general | solution.py:10
  140.2 19.6 %all-gather.21.cloned.1.call-done = bf16[1,1024,2560]{2,1,0:T(8,128)(2,1)} async-done(((bf16[1,128,2560]{2,1,0:T(8,128)(2,1)}), bf16[1,1024,2560]{2,1,0:T(8,128)(2,1)}) %all-gather.21.cloned.1.call-update) | async-done | bytes 5242896 | tf_op jit(solution)/shard_map/all_gather | solution.py:21
  159.8 18.4 %fusion.26 = f32[2048,2560]{1,0:T(8,128)} fusion(bf16[1,1024,2560]{2,1,0:T(8,128)(2,1)} %all-gather.21.cloned.1.call-done, bf16[2048,1024]{0,1:T(8,128)(2,1)} %get-tuple-element.21, f32[2048]{0:T(1024)S(1)} %add_rsqrt_fusion), kind=kOutput, calls=%fused_computation.53 | convolution fusion | flops 10743709696 | bytes 30416896 | tf_op jit(solution)/shard_map/dot_general | solution.py:10
  178.2 19.0 %all-gather.23.cloned.1.call-done = bf16[1,1024,2560]{2,1,0:T(8,128)(2,1)} async-done(((bf16[1,128,2560]{2,1,0:T(8,128)(2,1)}), bf16[1,1024,2560]{2,1,0:T(8,128)(2,1)}) %all-gather.23.cloned.1.call-update) | async-done | bytes 5242896 | tf_op jit(solution)/shard_map/all_gather | solution.py:21
  197.2 18.4 %fusion.22 = f32[2048,2560]{1,0:T(8,128)} fusion(bf16[1,1024,2560]{2,1,0:T(8,128)(2,1)} %all-gather.23.cloned.1.call-done, bf16[2048,1024]{0,1:T(8,128)(2,1)} %get-tuple-element.21, f32[2048]{0:T(1024)S(1)} %add_rsqrt_fusion), kind=kOutput, calls=%fused_computation.49 | convolution fusion | flops 10743709696 | bytes 30416896 | tf_op jit(solution)/shard_map/dot_general | solution.py:10
  215.6 18.5 %all-gather.19.cloned.1.call-done = bf16[1,2560,1024]{2,1,0:T(8,128)(2,1)} async-done(((bf16[1,320,1024]{2,1,0:T(8,128)(2,1)}), bf16[1,2560,1024]{2,1,0:T(8,128)(2,1)}) %all-gather.19.cloned.1.call-update) | async-done | bytes 5242896 | tf_op jit(solution)/shard_map/all_gather | solution.py:21
  234.0 32.0 %fusion.2 = (bf16[2048,2560]{1,0:T(8,128)(2,1)}, bf16[2048,2560]{1,0:T(8,128)(2,1)}) fusion(f32[2048,2560]{1,0:T(8,128)} %fusion.22, f32[2048,2560]{1,0:T(8,128)} %fusion.26, bf16[1,2560,1024]{2,1,0:T(8,128)(2,1)} %all-gather.19.cloned.1.call-done, bf16[1,2048,1024]{2,1,0:T(8,128)(2,1)} %param.6), kind=kOutput, calls=%fused_computation.6 | convolution fusion | flops 10816061440 | bytes 72351744 | tf_op jit(solution)/shard_map/dot_general | solution.py:10
  266.1 17.3 %fusion.20 = f32[2048,1024]{0,1:T(8,128)} fusion(bf16[2048,2560]{1,0:T(8,128)(2,1)} %get-tuple-element.11, bf16[1,1024,2560]{2,1,0:T(8,128)(2,1)} %all-gather.23.cloned.1.call-done), kind=kOutput, calls=%fused_computation.47 | convolution fusion | flops 10737418240 | bytes 24117248 | tf_op jit(solution)/shard_map/dot_general | solution.py:10
  283.4 16.9 %fusion.18 = (f32[2048]{0:T(1024)S(1)}, bf16[2048,1024]{0,1:T(8,128)(2,1)S(1)}) fusion(bf16[2048,1024]{0,1:T(8,128)(2,1)S(1)} %copy-done.5, f32[2048,1024]{0,1:T(8,128)} %fusion.20, bf16[2048,2560]{1,0:T(8,128)(2,1)} %get-tuple-element.10, bf16[1,1024,2560]{2,1,0:T(8,128)(2,1)} %all-gather.21.cloned.1.call-done), kind=kOutput, calls=%fused_computation.38 | convolution fusion | flops 10749999104 | bytes 32514048 | tf_op jit(solution)/shard_map/dot_general | solution.py:10
  300.3 3.7 fusion.42
  304.0 2.0 copy-done.2
  306.1 15.4 %convolution_convert_fusion.2 = bf16[2560,1024]{1,0:T(8,128)(2,1)} fusion(bf16[2048,2560]{1,0:T(8,128)(2,1)} %get-tuple-element.18, bf16[2048,1024]{0,1:T(8,128)(2,1)S(1)} %fusion.42), kind=kOutput, calls=%fused_computation.42 | convolution fusion | flops 10740039680 | bytes 19922944 | tf_op jit(solution)/shard_map/dot_general | solution.py:10
  321.5 0.0 reduce-scatter.15.cloned.1.call-update
  321.5 0.0 reduce-scatter.17.cloned.1.call-start
  321.5 22.1 %fusion.19 = bf16[2560,1024]{1,0:T(8,128)(2,1)} fusion(f32[2048,2560]{1,0:T(8,128)} %fusion.26, bf16[1,2048,1024]{2,1,0:T(8,128)(2,1)} %param.6, f32[2048,2560]{1,0:T(8,128)} %fusion.22), kind=kOutput, calls=%fused_computation.41 | convolution fusion | flops 10771496960 | bytes 51380224 | tf_op jit(solution)/shard_map/dot_general | solution.py:10
  343.6 0.0 reduce-scatter.17.cloned.1.call-update
  343.6 0.0 reduce-scatter.13.cloned.1.call-start
  343.7 16.5 %convolution_convert_fusion.3 = bf16[1024,2560]{1,0:T(8,128)(2,1)} fusion(bf16[2048,2560]{1,0:T(8,128)(2,1)} %get-tuple-element.10, bf16[2048,1024]{0,1:T(8,128)(2,1)} %get-tuple-element.21, f32[2048]{0:T(1024)S(1)} %add_rsqrt_fusion), kind=kOutput, calls=%fused_computation.43 | convolution fusion | flops 10746331136 | bytes 19931136 | tf_op jit(solution)/shard_map/dot_general | solution.py:10
  360.2 0.0 reduce-scatter.13.cloned.1.call-update
  360.2 0.0 reduce-scatter.11.cloned.1.call-start
  360.3 31.9 %fusion.4 = (bf16[2048,2560]{1,0:T(8,128)(2,1)}, bf16[2048,2560]{1,0:T(8,128)(2,1)}) fusion(f32[2048,2560]{1,0:T(8,128)} %get-tuple-element.19, f32[2048,2560]{1,0:T(8,128)} %fusion.38, bf16[2048,1024]{0,1:T(8,128)(2,1)} %copy-done.2, bf16[1,2560,1024]{2,1,0:T(8,128)(2,1)} %all-gather.17.cloned.1.call-done), kind=kOutput, calls=%fused_computation.8 | convolution fusion | flops 10816061440 | bytes 72351744 | tf_op jit(solution)/shard_map/dot_general | solution.py:10
  392.2 15.2 %convolution_convert_fusion.4 = bf16[1024,2560]{1,0:T(8,128)(2,1)} fusion(bf16[2048,2560]{1,0:T(8,128)(2,1)} %get-tuple-element.9, bf16[1,2048,1024]{1,2,0:T(8,128)(2,1)S(1)} %copy-done, f32[2048]{0:T(1024)S(1)} %copy-done.9), kind=kOutput, calls=%fused_computation.44 | convolution fusion | flops 10746331136 | bytes 19931136 | tf_op jit(solution)/shard_map/dot_general | solution.py:10
  407.5 0.0 reduce-scatter.11.cloned.1.call-update
  407.5 0.0 reduce-scatter.9.cloned.1.call-start
  407.6 16.5 %convolution_convert_fusion.5 = bf16[1024,2560]{1,0:T(8,128)(2,1)} fusion(bf16[2048,2560]{1,0:T(8,128)(2,1)} %get-tuple-element.11, bf16[2048,1024]{0,1:T(8,128)(2,1)} %get-tuple-element.21, f32[2048]{0:T(1024)S(1)} %add_rsqrt_fusion), kind=kOutput, calls=%fused_computation.45 | convolution fusion | flops 10746331136 | bytes 19931136 | tf_op jit(solution)/shard_map/dot_general | solution.py:10
  424.1 0.0 reduce-scatter.9.cloned.1.call-update
  424.1 0.0 reduce-scatter.7.cloned.1.call-start
  424.2 16.8 %convolution_convert_fusion.6 = bf16[1024,2560]{1,0:T(8,128)(2,1)} fusion(bf16[2048,2560]{1,0:T(8,128)(2,1)} %get-tuple-element.8, bf16[1,2048,1024]{1,2,0:T(8,128)(2,1)} %copy.10, f32[2048]{0:T(1024)S(1)} %copy-done.9), kind=kOutput, calls=%fused_computation.46 | convolution fusion | flops 10746331136 | bytes 19931136 | tf_op jit(solution)/shard_map/dot_general | solution.py:10
  440.9 0.0 reduce-scatter.7.cloned.1.call-update
  441.0 17.4 %fusion.32 = f32[2048,1024]{0,1:T(8,128)} fusion(bf16[2048,2560]{1,0:T(8,128)(2,1)} %get-tuple-element.9, bf16[1,1024,2560]{2,1,0:T(8,128)(2,1)} %all-gather.15.cloned.1.call-done), kind=kOutput, calls=%fused_computation.59 | convolution fusion | flops 10737418240 | bytes 24117248 | tf_op jit(solution)/shard_map/dot_general | solution.py:10
  458.3 16.9 %fusion.15 = (f32[2048]{0:T(1024)S(1)}, bf16[2048,1024]{0,1:T(8,128)(2,1)S(1)}) fusion(bf16[1,2048,1024]{1,2,0:T(8,128)(2,1)S(1)} %copy-done.1, f32[2048,1024]{0,1:T(8,128)} %fusion.32, bf16[2048,2560]{1,0:T(8,128)(2,1)} %get-tuple-element.8, bf16[1,1024,2560]{2,1,0:T(8,128)(2,1)} %all-gather.13.cloned.1.call-done), kind=kOutput, calls=%fused_computation.35 | convolution fusion | flops 10749999104 | bytes 32514048 | tf_op jit(solution)/shard_map/dot_general | solution.py:10
  475.3 4.6 fusion.41
  480.0 6.4 %copy.11 = bf16[1,2048,1024]{2,1,0:T(8,128)(2,1)} copy(bf16[1,2048,1024]{1,2,0:T(8,128)(2,1)} %fusion.41) | data formatting | bytes 8388608
  486.4 2.5 pad_maximum_fusion.2
  488.8 33.4 %reduce-scatter.11.cloned.1.call-done = bf16[128,2560]{1,0:T(8,128)(2,1)} async-done(((bf16[1024,2560]{1,0:T(8,128)(2,1)}), bf16[128,2560]{1,0:T(8,128)(2,1)}) %reduce-scatter.11.cloned.1.call-update) | async-done | bytes 655376 | tf_op jit(solution)/shard_map/reduce_scatter | solution.py:24
  522.3 2.5 pad_maximum_fusion.1
  524.7 48.6 %reduce-scatter.9.cloned.1.call-done = bf16[128,2560]{1,0:T(8,128)(2,1)} async-done(((bf16[1024,2560]{1,0:T(8,128)(2,1)}), bf16[128,2560]{1,0:T(8,128)(2,1)}) %reduce-scatter.9.cloned.1.call-update) | async-done | bytes 655376 | tf_op jit(solution)/shard_map/reduce_scatter | solution.py:24
  573.3 50.9 %reduce-scatter.7.cloned.1.call-done = bf16[128,2560]{1,0:T(8,128)(2,1)} async-done(((bf16[1024,2560]{1,0:T(8,128)(2,1)}), bf16[128,2560]{1,0:T(8,128)(2,1)}) %reduce-scatter.7.cloned.1.call-update) | async-done | bytes 655376 | tf_op jit(solution)/shard_map/reduce_scatter | solution.py:24
  624.2 2.5 pad_maximum_fusion
  (25 shorter events, 0.1 us)
Async XLA Ops:
  7.2 41.2 %all-gather.13.cloned.1.call-start = ((), (), s32[]{:S(2)}) async-start(), calls=%async_computation.12 | async-start | bytes 5898240 | tf_op jit(solution)/shard_map/all_gather | solution.py:21
  9.7 75.7 %all-gather.15.cloned.1.call-start = ((), (), s32[]{:S(2)}) async-start(), calls=%async_computation.13 | async-start | bytes 5898240 | tf_op jit(solution)/shard_map/all_gather | solution.py:21
  12.2 110.2 %all-gather.17.cloned.1.call-start = ((), (), s32[]{:S(2)}) async-start(), calls=%async_computation.14 | async-start | bytes 5898240 | tf_op jit(solution)/shard_map/all_gather | solution.py:21
  14.7 145.1 %all-gather.21.cloned.1.call-start = ((), (), s32[]{:S(2)}) async-start(), calls=%async_computation.16 | async-start | bytes 5898240 | tf_op jit(solution)/shard_map/all_gather | solution.py:21
  15.3 181.9 %all-gather.23.cloned.1.call-start = ((), (), s32[]{:S(2)}) async-start(), calls=%async_computation.17 | async-start | bytes 5898240 | tf_op jit(solution)/shard_map/all_gather | solution.py:21
  15.9 218.2 %all-gather.19.cloned.1.call-start = ((), (), s32[]{:S(2)}) async-start(), calls=%async_computation.15 | async-start | bytes 5898240 | tf_op jit(solution)/shard_map/all_gather | solution.py:21
  16.4 469.9 %reduce-scatter.15.cloned.1.call-start = ((), (), s32[]{:S(2)}) async-start(), calls=%async_computation.10 | async-start | bytes 5898240 | tf_op jit(solution)/shard_map/reduce_scatter | solution.py:24
  26.0 0.6 copy-start.6
  26.6 58.8 %copy-start.8 = (f32[2048]{0:T(1024)}, f32[2048]{0:T(1024)S(1)}, u32[]{:S(2)}) copy-start(f32[2048]{0:T(1024)S(1)} %add_rsqrt_fusion.1) | copy-start | bytes 24580
  266.1 17.3 %copy-start.5 = (bf16[2048,1024]{0,1:T(8,128)(2,1)S(1)}, bf16[2048,1024]{0,1:T(8,128)(2,1)}, u32[]{:S(2)}) copy-start(bf16[2048,1024]{0,1:T(8,128)(2,1)} %get-tuple-element.21) | copy-start | bytes 12582916
  283.4 16.9 %copy-start.4 = (bf16[1,2048,1024]{1,2,0:T(8,128)(2,1)S(1)}, bf16[1,2048,1024]{1,2,0:T(8,128)(2,1)}, u32[]{:S(2)}) copy-start(bf16[1,2048,1024]{1,2,0:T(8,128)(2,1)} %copy.9) | copy-start | bytes 12582916
  304.0 2.1 copy-start.2
  321.5 164.9 %reduce-scatter.17.cloned.1.call-start = ((), (), s32[]{:S(2)}) async-start(), calls=%async_computation.11 | async-start | bytes 5898240 | tf_op jit(solution)/shard_map/reduce_scatter | solution.py:24
  343.6 145.2 %reduce-scatter.13.cloned.1.call-start = ((), (), s32[]{:S(2)}) async-start(), calls=%async_computation.9 | async-start | bytes 5898240 | tf_op jit(solution)/shard_map/reduce_scatter | solution.py:24
  360.2 162.0 %reduce-scatter.11.cloned.1.call-start = ((), (), s32[]{:S(2)}) async-start(), calls=%async_computation.8 | async-start | bytes 5898240 | tf_op jit(solution)/shard_map/reduce_scatter | solution.py:24
  360.3 31.9 %copy-start = (bf16[1,2048,1024]{1,2,0:T(8,128)(2,1)S(1)}, bf16[1,2048,1024]{1,2,0:T(8,128)(2,1)}, u32[]{:S(2)}) copy-start(bf16[1,2048,1024]{1,2,0:T(8,128)(2,1)} %copy.10) | copy-start | bytes 12582916
  360.3 31.9 %copy-start.9 = (f32[2048]{0:T(1024)S(1)}, f32[2048]{0:T(1024)}, u32[]{:S(2)}) copy-start(f32[2048]{0:T(1024)} %copy-done.8) | copy-start | bytes 24580
  407.5 165.8 %reduce-scatter.9.cloned.1.call-start = ((), (), s32[]{:S(2)}) async-start(), calls=%async_computation.7 | async-start | bytes 5898240 | tf_op jit(solution)/shard_map/reduce_scatter | solution.py:24
  424.1 200.0 %reduce-scatter.7.cloned.1.call-start = ((), (), s32[]{:S(2)}) async-start(), calls=%async_computation.6 | async-start | bytes 5898240 | tf_op jit(solution)/shard_map/reduce_scatter | solution.py:24
  440.9 17.4 %copy-start.1 = (bf16[1,2048,1024]{1,2,0:T(8,128)(2,1)S(1)}, bf16[1,2048,1024]{1,2,0:T(8,128)(2,1)}, u32[]{:S(2)}) copy-start(bf16[1,2048,1024]{1,2,0:T(8,128)(2,1)} %copy.10) | copy-start | bytes 12582916
  458.3 16.9 %copy-start.7 = (f32[2048]{0:T(1024)S(1)}, f32[2048]{0:T(1024)}, u32[]{:S(2)}) copy-start(f32[2048]{0:T(1024)} %copy-done.6) | copy-start | bytes 24580
  458.3 17.0 %copy-start.3 = (bf16[2048,1024]{0,1:T(8,128)(2,1)S(1)}, bf16[2048,1024]{0,1:T(8,128)(2,1)}, u32[]{:S(2)}) copy-start(bf16[2048,1024]{0,1:T(8,128)(2,1)} %copy-done.2) | copy-start | bytes 12582916
Sparse Core Ops, SparseCore 0:
  10.4 37.9 all-gather.12
  50.2 35.1 all-gather.14
  87.2 35.1 all-gather.16
  124.6 35.1 all-gather.20
  162.0 35.1 all-gather.22
  198.9 35.1 all-gather.18
  321.6 47.6 reduce-scatter.14
  372.7 47.6 reduce-scatter.16
  423.7 47.6 reduce-scatter.12
  474.5 47.6 reduce-scatter.10
  525.6 47.6 reduce-scatter.8
  576.4 47.6 reduce-scatter.6

commit v2 on v0

v2 whole, which is shorter than its diff:
```python
import functools

import jax
import jax.numpy as jnp
from jax import lax
from jax.experimental import pallas as pl
from jax.experimental.pallas import tpu as pltpu
from jax.sharding import PartitionSpec as P

F32, BF16 = jnp.float32, jnp.bfloat16
T, D, FF, L, N = 2048, 1024, 2560, 2, 8
NC = 5
HC = FF // NC
SEG = HC // N
RD = D // N
K = L * NC
TT = 512
NT = T // TT
TE = 256
NN = (((1,), (0,)), ((), ()))
NT_DIMS = (((1,), (1,)), ((), ()))


def dot(a, b):
    return lax.dot_general(a, b, NN, preferred_element_type=F32)


def dot_nt(a, b):
    return lax.dot_general(a, b, NT_DIMS, preferred_element_type=F32)


def kernel(
    x_hbm, dy_hbm, own,
    dx_hbm, out, land,
    xh, a_ref, at_ref, dh, acc, wgu, wdn, pt, dg, du,
    keep, send0, recv0, s1, r1, s2, r2, outb,
    ag_send, ag_recv, rs_send, rs_recv, gu_sem, wd_sem, io_sem, out_sem,
):
    me = lax.axis_index("dp")
    core = me % 2
    ypos = (me // 2) % 2
    xpos = me // 4
    xn = (1 - xpos) * 4 + ypos * 2 + core
    yn = xpos * 4 + (1 - ypos) * 2 + core
    cn = xpos * 4 + ypos * 2 + (1 - core)
    diag = (1 - xpos) * 4 + (1 - ypos) * 2 + core
    q_me, q_x, q_y, q_d = me // 2, xn // 2, yn // 2, diag // 2

    def remote(src, dst, ssem, rsem, dev):
        return pltpu.make_async_remote_copy(
            src_ref=src, dst_ref=dst, send_sem=ssem, recv_sem=rsem,
            device_id={"dp": dev}, device_id_type=pl.DeviceIdType.MESH,
        )

    LO, HI = pl.ds(0, RD // 2), pl.ds(RD // 2, RD // 2)

    def ag(k, m, arriving=False):
        if m < 3:
            dev, src, dst, got = (xn, yn, cn)[m], own.at[k], land.at[k, me], land.at[k, (xn, yn, cn)[m]]
        elif m == 3:
            dev, src, dst, got = yn, land.at[k, xn, :, LO], land.at[k, xn, :, LO], land.at[k, diag, :, LO]
        elif m == 4:
            dev, src, dst, got = xn, land.at[k, yn, :, HI], land.at[k, yn, :, HI], land.at[k, diag, :, HI]
        else:
            b = (xn, yn, diag)[m - 5]
            there = (b // 2) * 2 + (1 - core)
            dev, src, dst, got = cn, land.at[k, b], land.at[k, b], land.at[k, there]
        if arriving:
            src = dst = got
        return remote(src, dst, ag_send.at[k, m], ag_recv.at[k, m], dev)

    def ag_start(k, ms):
        for m in ms:
            ag(k, m).start()

    def ag_wait(k, ms):
        for m in ms:
            ag(k, m, True).wait_recv()

    def load(p):
        k, slot = p % K, p % 2
        for r in range(N):
            if r == 0:
                j, src = me, own.at[k]
            else:
                fx, fy, fc = r // 4, (r // 2) % 2, r % 2
                j = ((xpos + fx) % 2) * 4 + ((ypos + fy) % 2) * 2 + (core + fc) % 2
                src = land.at[k, j]
            rows, segs = pl.ds(j * RD, RD), pl.ds(j * SEG, SEG)
            pltpu.make_async_copy(src.at[pl.ds(0, 2)], wgu.at[slot, :, rows, :], gu_sem.at[slot]).start()
            for h in range(2):
                pltpu.make_async_copy(
                    src.at[2, pl.ds(h * SEG, SEG)], wdn.at[slot, segs, pl.ds(h * HC, HC)], wd_sem.at[slot]
                ).start()

    def load_wait(p):
        slot = p % 2
        pltpu.make_async_copy(wgu.at[slot], wgu.at[slot], gu_sem.at[slot]).wait()
        pltpu.make_async_copy(wdn.at[slot], wdn.at[slot], wd_sem.at[slot]).wait()

    def tick(t):
        @pl.when(t < K)
        def _():
            ag_wait(t, (0, 1))
            ag_start(t, (3, 4, 5, 6))

        @pl.when(t + 2 < K)
        def _():
            ag_start(t + 2, (0, 1, 2))

        @pl.when((t >= 1) & (t - 1 < K))
        def _():
            ag_wait(t - 1, (3, 4))
            ag_start(t - 1, (7,))
            ag_wait(t - 1, (2, 5, 6, 7))

        @pl.when((t >= 1) & (t - 1 < K + NC))
        def _():
            load(t - 1)

    def rs(v, m):
        src, dst, dev = (
            (send0, recv0.at[v], cn),
            (s1.at[0], r1.at[v, 0], xn),
            (s1.at[1], r1.at[v, 1], yn),
            (s2.at[0], r2.at[v, 0], xn),
            (s2.at[1], r2.at[v, 1], yn),
        )[m]
        return remote(src, dst, rs_send.at[m], rs_recv.at[v, m], dev)

    def half(q, h):
        return pl.ds(q * RD + h * (RD // 2), RD // 2)

    def block(q):
        return pl.ds(q * RD, RD)

    def f1(b):
        v = b % 2
        rs(v, 0).wait_recv()

        @pl.when(b >= 1)
        def _():
            rs(v, 1).wait_send()
            rs(v, 2).wait_send()

        for i in range(3):
            keep[v, i] = keep[v, i] + recv0[v, i].astype(F32)
        for i in range(3):
            s1[0, i] = keep[v, i, half(q_d, 0), :].astype(BF16)
            s1[1, i] = keep[v, i, half(q_d, 1), :].astype(BF16)
        rs(v, 1).start()
        rs(v, 2).start()

    def f2(b):
        v = b % 2
        rs(v, 1).wait_recv()
        rs(v, 2).wait_recv()

        @pl.when(b >= 1)
        def _():
            rs(v, 3).wait_send()
            rs(v, 4).wait_send()

        for i in range(3):
            keep[v, i, half(q_y, 0), :] = keep[v, i, half(q_y, 0), :] + r1[v, 0, i].astype(F32)
            keep[v, i, half(q_x, 1), :] = keep[v, i, half(q_x, 1), :] + r1[v, 1, i].astype(F32)
        for i in range(3):
            s2[0, i] = keep[v, i, block(q_x), :].astype(BF16)
            s2[1, i] = keep[v, i, block(q_y), :].astype(BF16)
        rs(v, 3).start()
        rs(v, 4).start()

    def out_copy(b):
        return pltpu.make_async_copy(outb, out.at[(b + NC) % K], out_sem)

    def f3(b):
        v = b % 2
        rs(v, 3).wait_recv()
        rs(v, 4).wait_recv()

        @pl.when(b >= 1)
        def _():
            out_copy(b - 1).wait()

        for i in range(3):
            total = keep[v, i, block(q_me), :] + r2[v, 0, i].astype(F32) + r2[v, 1, i].astype(F32)
            outb[i] = total.astype(BF16)
        out_copy(b).start()

    def norm_tile(i):
        rows = pl.ds(pl.multiple_of(i * TE, TE), TE)
        wide = xh[rows, :].astype(F32)
        scale = lax.rsqrt(jnp.mean(wide * wide, -1, keepdims=True) + 1e-6)
        a = (wide * scale).astype(BF16)
        a_ref[rows, :] = a
        across = a.T
        for j in range(N):
            place = ((j % 2 + core) % 2) * (N // 2) + j // 2
            at_ref[pl.ds(place * RD, RD), rows] = across[j * RD : (j + 1) * RD, :]
        acc[rows, :] = jnp.zeros((TE, D), F32)

    def norm_back(i, store):
        rows = pl.ds(pl.multiple_of(i * TE, TE), TE)
        wide = xh[rows, :].astype(F32)
        scale = lax.rsqrt(jnp.mean(wide * wide, -1, keepdims=True) + 1e-6)
        da = acc[rows, :].astype(BF16).astype(F32)
        inner = jnp.mean(da * wide, -1, keepdims=True)
        back = (scale * da - wide * (scale * scale * scale * inner)).astype(BF16)
        store(rows, (dh[rows, :].astype(F32) + back.astype(F32)).astype(BF16))

    def loop(n, f):
        lax.fori_loop(0, n, lambda i, _: (f(i), 0)[1], 0)

    barrier = pltpu.get_barrier_semaphore()
    for dev in (xn, yn, cn):
        pl.semaphore_signal(barrier, inc=1, device_id={"dp": dev}, device_id_type=pl.DeviceIdType.MESH)
    x_copy = pltpu.make_async_copy(x_hbm, xh, io_sem.at[0])
    dy_copy = pltpu.make_async_copy(dy_hbm, dh, io_sem.at[1])
    x_copy.start()
    dy_copy.start()
    pl.semaphore_wait(barrier, 3)
    ag_start(0, (0, 1, 2))
    ag_start(1, (0, 1, 2))
    x_copy.wait()
    loop(T // TE, norm_tile)

    def forward(slot):
        def tile(i):
            rows = pl.ds(pl.multiple_of(i * TT, TT), TT)
            a = a_ref[rows, :]
            gate = dot(a, wgu[slot, 0])
            up = dot(a, wgu[slot, 1])
            p = (gate * jax.nn.sigmoid(gate) * up).astype(BF16)
            acc[rows, :] = acc[rows, :] + dot(p, wdn[slot])

        loop(NT, tile)

    def first(t):
        tick(t)

        @pl.when(t >= 2)
        def _():
            load_wait(t - 2)
            forward(t % 2)

    loop(NC + 2, first)

    def next_state(i):
        rows = pl.ds(pl.multiple_of(i * TE, TE), TE)
        xh[rows, :] = (xh[rows, :].astype(F32) + acc[rows, :].astype(BF16).astype(F32)).astype(BF16)
        norm_tile(i)

    loop(T // TE, next_state)
    dy_copy.wait()

    def backward(s):
        tick(s + NC + 2)
        load_wait(s + NC)
        slot = (s + NC) % 2
        v = s % 2

        @pl.when(s >= 2)
        def _():
            f3(s - 2)

        def tile(i):
            @pl.when((i == 1) & (s >= 1))
            def _():
                f1(s - 1)

            rows = pl.ds(pl.multiple_of(i * TT, TT), TT)
            a = a_ref[rows, :]
            gate = dot(a, wgu[slot, 0])
            up = dot(a, wgu[slot, 1])
            dp = dot_nt(dh[rows, :], wdn[slot]).astype(BF16).astype(F32)
            sig = jax.nn.sigmoid(gate)
            act = gate * sig
            du[rows, :] = (dp * act).astype(BF16)
            dg[rows, :] = (dp * up * (sig + act * (1.0 - sig))).astype(BF16)
            across = (act * up).astype(BF16).T
            for j in range(N):
                place = ((j % 2 + core) % 2) * (N // 2) + j // 2
                pt[pl.ds(place * SEG, SEG), rows] = across[j * SEG : (j + 1) * SEG, :]

        loop(NT, tile)

        @pl.when(s >= 1)
        def _():
            f2(s - 1)
            rs(v, 0).wait_send()

        top, low = pl.ds(0, D // 2), pl.ds(D // 2, D // 2)
        for i, d in enumerate((dg, du)):
            send0[i] = dot(at_ref[low, :], d[...]).astype(BF16)
            keep[v, i] = dot(at_ref[top, :], d[...])
        theirs = dot(pt[pl.ds(HC // 2, HC // 2), :], dh[...]).astype(BF16)
        ours = dot(pt[pl.ds(0, HC // 2), :], dh[...])
        for q in range(N // 2):
            for h in range(2):
                to = pl.ds(q * RD + h * SEG, SEG)
                send0[2, to, :] = theirs[q * SEG : (q + 1) * SEG, h * HC : (h + 1) * HC]
                keep[v, 2, to, :] = ours[q * SEG : (q + 1) * SEG, h * HC : (h + 1) * HC]
        rs(v, 0).start()

        def da_tile(i):
            rows = pl.ds(pl.multiple_of(i * TT, TT), TT)
            acc[rows, :] = acc[rows, :] + (dot_nt(dg[rows, :], wgu[slot, 0]) + dot_nt(du[rows, :], wgu[slot, 1]))

        loop(NT, da_tile)

        @pl.when(s == NC - 1)
        def _():
            def keep_dh(rows, value):
                dh[rows, :] = value

            loop(T // TE, lambda i: norm_back(i, keep_dh))
            again = pltpu.make_async_copy(x_hbm, xh, io_sem.at[0])
            again.start()
            again.wait()
            loop(T // TE, norm_tile)

    loop(K, backward)

    f3(K - 2)
    f1(K - 1)

    def keep_dx(rows, value):
        a_ref[rows, :] = value

    loop(T // TE, lambda i: norm_back(i, keep_dx))
    dx_copy = pltpu.make_async_copy(a_ref, dx_hbm, io_sem.at[1])
    dx_copy.start()
    f2(K - 1)
    f3(K - 1)
    out_copy(K - 1).wait()
    dx_copy.wait()
    for m in range(5):
        rs(1, m).wait_send()

    def drain(k):
        for m in range(8):
            ag(k, m).wait_send()

    loop(K, drain)


def mlp_stack(x, dy, own):
    any_space = pl.BlockSpec(memory_space=pl.ANY)
    vm = pltpu.VMEM
    flops = 19 * 2 * T * D * FF
    return pl.pallas_call(
        kernel,
        name="mlp_stack",
        out_shape=[
            jax.ShapeDtypeStruct((T, D), BF16),
            jax.ShapeDtypeStruct((K, 3, RD, HC), BF16),
            jax.ShapeDtypeStruct((K, N, 3, RD, HC), BF16),
        ],
        in_specs=[any_space] * 3,
        out_specs=[any_space] * 3,
        scratch_shapes=[
            vm((T, D), BF16), vm((T, D), BF16), vm((D, T), BF16), vm((T, D), BF16), vm((T, D), F32),
            vm((2, 2, D, HC), BF16), vm((2, HC, D), BF16),
            vm((HC, T), BF16), vm((T, HC), BF16), vm((T, HC), BF16),
            vm((2, 3, D // 2, HC), F32), vm((3, D // 2, HC), BF16), vm((2, 3, D // 2, HC), BF16),
            vm((2, 3, RD // 2, HC), BF16), vm((2, 2, 3, RD // 2, HC), BF16),
            vm((2, 3, RD, HC), BF16), vm((2, 2, 3, RD, HC), BF16), vm((3, RD, HC), BF16),
            pltpu.SemaphoreType.DMA((K, 8)), pltpu.SemaphoreType.DMA((K, 8)),
            pltpu.SemaphoreType.DMA((5,)), pltpu.SemaphoreType.DMA((2, 5)),
            pltpu.SemaphoreType.DMA((2,)), pltpu.SemaphoreType.DMA((2,)),
            pltpu.SemaphoreType.DMA((2,)), pltpu.SemaphoreType.DMA,
        ],
        compiler_params=pltpu.CompilerParams(
            collective_id=0, has_side_effects=True, vmem_limit_bytes=67_000_000
        ),
        cost_estimate=pl.CostEstimate(flops=flops, bytes_accessed=10**8, transcendentals=T * FF),
    )(x, dy, own)


def solution(mesh):
    def body(x, dy, wg, wu, wd):
        def cut(w):
            return w.reshape(L, RD, N, NC, SEG).transpose(0, 3, 1, 2, 4).reshape(K, RD, HC)

        down = wd.reshape(L, NC, SEG, 2, HC).transpose(0, 1, 3, 2, 4).reshape(K, RD, HC)
        own = jnp.stack([cut(wg), cut(wu), down], axis=1)
        dx, out, _ = mlp_stack(x[0], dy[0], own)

        def join(g):
            return g.reshape(L, NC, RD, N, SEG).transpose(0, 2, 3, 1, 4).reshape(L, RD, FF)

        by_d = out[:, 2].reshape(L, NC, 2, SEG, HC).transpose(0, 1, 3, 2, 4).reshape(L, FF // N, D)
        return dx[None], join(out[:, 0]), join(out[:, 1]), by_d

    act = P(("rep", "dp"), None, None)
    w = P(None, "dp", None)
    return jax.shard_map(
        body, mesh=mesh, in_specs=(act, act, w, w, w), out_specs=(act, *[P("rep", "dp", None)] * 3), check_vma=False
    )
```

time: 752 us -> 379 us (0.50)
  Pallas kernels: 0 us -> 349 us
  matrix products: 319 us -> 0 us
  waiting for transfers between devices: 299 us -> 0 us
  other arithmetic: 75.2 us -> 2.13 us
  between operations: 14.7 us -> 0.75 us
  local copies, waits for them, and re-layouts: 36.7 us -> 26.7 us
    pallas_call x0 -> x1, Pallas kernels: none -> 349 us  [mlp_stack(): pl.pallas_call(kernel, name='mlp_stack', out_shape=[jax.ShapeDtypeStruct(...]
    dot_general x17 -> x0, matrix products: 319 us -> none  [the longest x6 123 us: layer(): up = jnp.dot(a, w['w_up'], preferred_element_type=jnp.float32)]
    unnamed x18 -> x0, waiting for transfers between devices: 224 us -> none
    squeeze x6 -> x0, waiting for transfers between devices: 75.5 us -> none  [stack(): h = layer(h, {name: w[number] for name, w in weights.items()})]
    unnamed x3 -> x0, other arithmetic: 52.3 us -> none
    unnamed x37 -> x9, local copies, waits for them, and re-layouts: 29.3 us -> 11.1 us
    add_any x2 -> x0, other arithmetic: 10.1 us -> none  [normed(): wide = h.astype(jnp.float32)]
    broadcast_in_dim x6 -> x0, other arithmetic: 8.34 us -> none  [stack(): h = layer(h, {name: w[number] for name, w in weights.items()})]
  transfers between devices with their start and end apart: 12 -> 0, of which waited for: 9 -> 0; matrix products, arithmetic and copies ran while one was open for 56% -> 0% of each run, Pallas kernels for 0% -> 0%
where the time goes in v2:
time: 379 us
  Pallas kernels  349 us (92%)
  local copies, waits for them, and re-layouts  26.7 us (7%)
    pallas_call x1, Pallas kernels, mlp_stack(): pl.pallas_call(kernel, name='mlp_stack', out_shape=[jax.ShapeDtypeStruct(...  349 us
    unnamed x9, local copies, waits for them, and re-layouts  11.1 us

profile of v2, /device:TPU:0, one launch (start us, length us, event | category | flops | bytes accessed | tf_op | source)
XLA Modules:
  0.0 378.7 jit_solution(3897441675061208567)
XLA Ops:
  0.6 1.8 copy.15
  2.4 0.1 copy.16
  2.5 0.0 copy-start.1
  2.5 1.4 copy.20
  4.0 0.0 copy-done.1
  4.0 0.8 copy.17
  4.8 0.1 copy.18
  4.9 0.6 copy.21
  5.5 3.6 reshape.28
  9.1 0.0 copy-start
  9.1 0.3 copy.19
  9.4 1.0 copy-done
  10.4 2.1 pad_maximum_fusion.own
  12.6 349.2 %mlp_stack.1 = (bf16[2048,1024]{1,0:T(8,128)(2,1)}, bf16[10,3,128,512]{3,2,1,0:T(8,128)(2,1)}, bf16[10,8,3,128,512]{4,3,2,1,0:T(8,128)(2,1)}) custom-call(bf16[2048,1024]{1,0:T(8,128)(2,1)} %bitcast.36, bf16[2048,1024]{1,0:T(8,128)(2,1)} %bitcast.37, bf16[10,3,128,512]{3,2,1,0:T(8,128)(2,1)} %pad_maximum_fusion.own), custom_call_target="tpu_custom_call" | custom-call | flops 204010946560 | bytes 100000000 | tf_op jit(solution)/shard_map/mlp_stack/pallas_call | solution.py:351
  361.7 3.6 fusion
  365.3 1.3 copy.26
  366.7 1.8 reshape.31
  368.4 0.8 copy.24
  369.2 0.1 copy.25
  369.3 1.4 copy.28
  370.8 1.8 copy.22
  372.5 0.1 copy.23
  372.7 1.4 copy.27
  374.1 4.6 %copy.30 = bf16[1,2048,1024]{2,1,0:T(8,128)(2,1)} copy(bf16[1,2048,1024]{2,1,0:T(8,128)(2,1)} %bitcast.35) | data formatting | bytes 8388608
Async XLA Ops:
  2.5 1.5 copy-start.1
  9.1 1.3 copy-start

commit v3 on v2

v3 whole, which is shorter than its diff:
```python
import jax
import jax.numpy as jnp
from jax import lax
from jax.experimental import pallas as pl
from jax.experimental.pallas import tpu as pltpu
from jax.sharding import PartitionSpec as P

F32, BF16 = jnp.float32, jnp.bfloat16
T, D, FF, L, N = 2048, 1024, 2560, 2, 8
NC = 5
HC = FF // NC
SEG = HC // N
RD = D // N
K = L * NC
TT = 512
TB = 1024
TE = 256
NN = (((1,), (0,)), ((), ()))
NT_DIMS = (((1,), (1,)), ((), ()))


def dot(a, b):
    return lax.dot_general(a, b, NN, preferred_element_type=F32)


def dot_nt(a, b):
    return lax.dot_general(a, b, NT_DIMS, preferred_element_type=F32)


def kernel(
    x_hbm, dy_hbm, own,
    dx_hbm, out, land, saved,
    xh, a_ref, at_ref, dh, acc, wgu, wdn, pt, dgu, gs,
    keep, mine, send0, recv0, s1, r1, s2, r2, outb,
    ag_send, ag_recv, rs_send, rs_recv, gu_sem, wd_sem, io_sem, out_sem, gs_sem,
):
    me = lax.axis_index("dp")
    core = me % 2
    ypos = (me // 2) % 2
    xpos = me // 4
    xn = (1 - xpos) * 4 + ypos * 2 + core
    yn = xpos * 4 + (1 - ypos) * 2 + core
    cn = xpos * 4 + ypos * 2 + (1 - core)
    diag = (1 - xpos) * 4 + (1 - ypos) * 2 + core
    q_me, q_x, q_y, q_d = me // 2, xn // 2, yn // 2, diag // 2

    def remote(src, dst, ssem, rsem, dev):
        return pltpu.make_async_remote_copy(
            src_ref=src, dst_ref=dst, send_sem=ssem, recv_sem=rsem,
            device_id={"dp": dev}, device_id_type=pl.DeviceIdType.MESH,
        )

    def loop(n, f):
        lax.fori_loop(0, n, lambda i, _: (f(i), 0)[1], 0)

    LO, HI = pl.ds(0, RD // 2), pl.ds(RD // 2, RD // 2)

    def ag(k, m, arriving=False):
        if m < 3:
            dev, src, dst, got = (xn, yn, cn)[m], own.at[k], land.at[k, me], land.at[k, (xn, yn, cn)[m]]
        elif m == 3:
            dev, src, dst, got = yn, land.at[k, xn, :, LO], land.at[k, xn, :, LO], land.at[k, diag, :, LO]
        elif m == 4:
            dev, src, dst, got = xn, land.at[k, yn, :, HI], land.at[k, yn, :, HI], land.at[k, diag, :, HI]
        else:
            b = (xn, yn, diag)[m - 5]
            there = (b // 2) * 2 + (1 - core)
            dev, src, dst, got = cn, land.at[k, b], land.at[k, b], land.at[k, there]
        if arriving:
            src = dst = got
        return remote(src, dst, ag_send.at[k, m], ag_recv.at[k, m], dev)

    def ag_start(k, ms):
        for m in ms:
            ag(k, m).start()

    def ag_wait(k, ms):
        for m in ms:
            ag(k, m, True).wait_recv()

    def load(p):
        k, slot = p % K, p % 2
        for r in range(N):
            if r == 0:
                j, src = me, own.at[k]
            else:
                fx, fy, fc = r // 4, (r // 2) % 2, r % 2
                j = ((xpos + fx) % 2) * 4 + ((ypos + fy) % 2) * 2 + (core + fc) % 2
                src = land.at[k, j]
            rows, segs = pl.ds(j * RD, RD), pl.ds(j * SEG, SEG)
            for h in range(2):
                cols = pl.ds(h * HC, HC)
                pltpu.make_async_copy(src.at[h], wgu.at[slot, rows, cols], gu_sem.at[slot]).start()
                pltpu.make_async_copy(
                    src.at[2, pl.ds(h * SEG, SEG)], wdn.at[slot, segs, cols], wd_sem.at[slot]
                ).start()

    def load_wait(p):
        slot = p % 2
        pltpu.make_async_copy(wgu.at[slot], wgu.at[slot], gu_sem.at[slot]).wait()
        pltpu.make_async_copy(wdn.at[slot], wdn.at[slot], wd_sem.at[slot]).wait()

    def tick(t):
        @pl.when(t < K)
        def _():
            ag_wait(t, (0, 1))
            ag_start(t, (3, 4, 5, 6))

        @pl.when(t + 2 < K)
        def _():
            ag_start(t + 2, (0, 1, 2))

        @pl.when((t >= 1) & (t - 1 < K))
        def _():
            ag_wait(t - 1, (3, 4))
            ag_start(t - 1, (7,))
            ag_wait(t - 1, (2, 5, 6, 7))

        @pl.when((t >= 1) & (t - 1 < K + NC))
        def _():
            load(t - 1)

    def rs(v, m):
        if m < 3:
            src, dst, dev = send0.at[m], recv0.at[v, m], cn
        else:
            i = (m - 3) % 2
            src, dst = (s1.at[i], r1.at[v, i]) if m < 5 else (s2.at[i], r2.at[v, i])
            dev = (xn, yn)[i]
        return remote(src, dst, rs_send.at[m], rs_recv.at[v, m], dev)

    def half(q, h):
        return pl.ds(q * RD + h * (RD // 2), RD // 2)

    def block(q):
        return pl.ds(q * RD, RD)

    def f1(b):
        v = b % 2

        @pl.when(b >= 1)
        def _():
            rs(v, 3).wait_send()
            rs(v, 4).wait_send()

        for i in range(3):
            rs(v, i).wait_recv()
            keep[i] = keep[i] + recv0[v, i].astype(F32)
            s1[0, i] = keep[i, half(q_d, 0), :].astype(BF16)
            s1[1, i] = keep[i, half(q_d, 1), :].astype(BF16)
        rs(v, 3).start()
        rs(v, 4).start()

    def f2(b):
        v = b % 2
        rs(v, 3).wait_recv()
        rs(v, 4).wait_recv()

        @pl.when(b >= 1)
        def _():
            rs(v, 5).wait_send()
            rs(v, 6).wait_send()

        for i in range(3):
            s2[0, i, LO, :] = keep[i, half(q_x, 0), :].astype(BF16)
            s2[0, i, HI, :] = (keep[i, half(q_x, 1), :] + r1[v, 1, i].astype(F32)).astype(BF16)
            s2[1, i, LO, :] = (keep[i, half(q_y, 0), :] + r1[v, 0, i].astype(F32)).astype(BF16)
            s2[1, i, HI, :] = keep[i, half(q_y, 1), :].astype(BF16)
        rs(v, 5).start()
        rs(v, 6).start()
        for i in range(3):
            mine[i] = keep[i, block(q_me), :]

    def out_copy(b):
        return pltpu.make_async_copy(outb, out.at[(b + NC) % K], out_sem)

    def f3(b):
        v = b % 2

        @pl.when(b >= 1)
        def _():
            out_copy(b - 1).wait()

        rs(v, 5).wait_recv()
        rs(v, 6).wait_recv()
        for i in range(3):
            outb[i] = (mine[i] + r2[v, 0, i].astype(F32) + r2[v, 1, i].astype(F32)).astype(BF16)
        out_copy(b).start()

    def some(i, n):
        return pl.ds(pl.multiple_of(i * n, n), n)

    def norm_tile(i):
        rows = some(i, TE)
        wide = xh[rows, :].astype(F32)
        scale = lax.rsqrt(jnp.mean(wide * wide, -1, keepdims=True) + 1e-6)
        a = (wide * scale).astype(BF16)
        a_ref[rows, :] = a
        across = a.T
        for j in range(N):
            place = ((j % 2 + core) % 2) * (N // 2) + j // 2
            at_ref[pl.ds(place * RD, RD), rows] = across[j * RD : (j + 1) * RD, :]
        acc[rows, :] = jnp.zeros((TE, D), F32)

    def norm_back(i, to):
        rows = some(i, TE)
        wide = xh[rows, :].astype(F32)
        scale = lax.rsqrt(jnp.mean(wide * wide, -1, keepdims=True) + 1e-6)
        da = acc[rows, :].astype(BF16).astype(F32)
        inner = jnp.mean(da * wide, -1, keepdims=True)
        back = (scale * da - wide * (scale * scale * scale * inner)).astype(BF16)
        to[rows, :] = (dh[rows, :].astype(F32) + back.astype(F32)).astype(BF16)

    barrier = pltpu.get_barrier_semaphore()
    for dev in (xn, yn, cn):
        pl.semaphore_signal(barrier, inc=1, device_id={"dp": dev}, device_id_type=pl.DeviceIdType.MESH)
    x_copy = pltpu.make_async_copy(x_hbm, xh, io_sem.at[0])
    dy_copy = pltpu.make_async_copy(dy_hbm, dh, io_sem.at[1])
    x_copy.start()
    dy_copy.start()
    pl.semaphore_wait(barrier, 3)
    ag_start(0, (0, 1, 2))
    ag_start(1, (0, 1, 2))
    x_copy.wait()
    loop(T // TE, norm_tile)

    NT = T // TT

    def saving(g):
        return pltpu.make_async_copy(gs.at[g % 2], saved.at[g], gs_sem.at[g % 2])

    def reading(g):
        return pltpu.make_async_copy(saved.at[g], gs.at[g % 2], gs_sem.at[g % 2])

    def first(t):
        tick(t)

        @pl.when(t >= 2)
        def _():
            c, slot = t - 2, t % 2
            load_wait(c)

            def tile(i):
                g = c * NT + i
                rows = some(i, TT)
                both = dot(a_ref[rows, :], wgu[slot])

                @pl.when(g >= 2)
                def _():
                    saving(g - 2).wait()

                gs[g % 2] = both
                saving(g).start()
                gate, up = both[:, :HC], both[:, HC:]
                p = (gate * jax.nn.sigmoid(gate) * up).astype(BF16)
                acc[rows, :] = acc[rows, :] + dot(p, wdn[slot])

            loop(NT, tile)

    loop(NC + 2, first)

    def next_state(i):
        rows = some(i, TE)
        xh[rows, :] = (xh[rows, :].astype(F32) + acc[rows, :].astype(BF16).astype(F32)).astype(BF16)
        norm_tile(i)

    loop(T // TE, next_state)
    dy_copy.wait()
    saving(NC * NT - 2).wait()
    saving(NC * NT - 1).wait()
    reading(0).start()
    reading(1).start()

    def backward(s, n, tile):
        tick(s + NC + 2)
        load_wait(s + NC)
        slot = (s + NC) % 2
        v = s % 2

        def step(i):
            tile(s, i, slot)

            @pl.when((i == 0) & (s >= 1))
            def _():
                f2(s - 1)

        loop(n, step)

        @pl.when(s >= 1)
        def _():
            for m in range(3):
                rs(v, m).wait_send()

        top, low = pl.ds(0, D // 2), pl.ds(D // 2, D // 2)
        both = dot(at_ref[low, :], dgu[...])
        for i in range(2):
            send0[i] = both[:, i * HC : (i + 1) * HC].astype(BF16)
            rs(v, i).start()
        down = dot(pt[pl.ds(HC // 2, HC // 2), :], dh[...])
        for q in range(N // 2):
            for h in range(2):
                to = pl.ds(q * RD + h * SEG, SEG)
                send0[2, to, :] = down[q * SEG : (q + 1) * SEG, h * HC : (h + 1) * HC].astype(BF16)
        rs(v, 2).start()
        both = dot(at_ref[top, :], dgu[...])
        for i in range(2):
            keep[i] = both[:, i * HC : (i + 1) * HC]
        down = dot(pt[pl.ds(0, HC // 2), :], dh[...])
        for q in range(N // 2):
            for h in range(2):
                to = pl.ds(q * RD + h * SEG, SEG)
                keep[2, to, :] = down[q * SEG : (q + 1) * SEG, h * HC : (h + 1) * HC]

        @pl.when(s >= 1)
        def _():
            f3(s - 1)

        f1(s)

        def da_tile(i):
            rows = some(i, TT)
            acc[rows, :] = acc[rows, :] + dot_nt(dgu[rows, :], wgu[slot])

        loop(NT, da_tile)

    def hidden(rows, gate, up, slot):
        dp = dot_nt(dh[rows, :], wdn[slot]).astype(BF16).astype(F32)
        sig = jax.nn.sigmoid(gate)
        act = gate * sig
        dgu[rows, pl.ds(HC, HC)] = (dp * act).astype(BF16)
        dgu[rows, pl.ds(0, HC)] = (dp * up * (sig + act * (1.0 - sig))).astype(BF16)
        across = (act * up).astype(BF16).T
        for j in range(N):
            place = ((j % 2 + core) % 2) * (N // 2) + j // 2
            pt[pl.ds(place * SEG, SEG), rows] = across[j * SEG : (j + 1) * SEG, :]

    def computed(s, i, slot):
        rows = some(i, TB)
        both = dot(a_ref[rows, :], wgu[slot])
        hidden(rows, both[:, :HC], both[:, HC:], slot)

    def read_back(s, i, slot):
        g = (s - NC) * NT + i
        reading(g).wait()
        hidden(some(i, TT), gs[g % 2, :, pl.ds(0, HC)], gs[g % 2, :, pl.ds(HC, HC)], slot)

        @pl.when(g + 2 < NC * NT)
        def _():
            reading(g + 2).start()

    loop(NC, lambda s: backward(s, T // TB, computed))

    def again(i):
        return pltpu.make_async_copy(x_hbm.at[some(i, TE)], xh.at[some(i, TE)], io_sem.at[0])

    def change(i):
        norm_back(i, dh)
        again(i).start()

    loop(T // TE, change)
    x_copy.wait()
    loop(T // TE, norm_tile)
    loop(NC, lambda s: backward(s + NC, NT, read_back))

    f2(K - 1)
    loop(T // TE, lambda i: norm_back(i, a_ref))
    dx_copy = pltpu.make_async_copy(a_ref, dx_hbm, io_sem.at[1])
    dx_copy.start()
    f3(K - 1)
    out_copy(K - 1).wait()
    dx_copy.wait()
    for m in range(7):
        rs(1, m).wait_send()

    def drain(k):
        for m in range(8):
            ag(k, m).wait_send()

    loop(K, drain)


def mlp_stack(x, dy, own):
    any_space = pl.BlockSpec(memory_space=pl.ANY)
    vm = pltpu.VMEM
    flops = 17 * 2 * T * D * FF
    return pl.pallas_call(
        kernel,
        name="mlp_stack",
        out_shape=[
            jax.ShapeDtypeStruct((T, D), BF16),
            jax.ShapeDtypeStruct((K, 3, RD, HC), BF16),
            jax.ShapeDtypeStruct((K, N, 3, RD, HC), BF16),
            jax.ShapeDtypeStruct((NC * (T // TT), TT, 2 * HC), F32),
        ],
        in_specs=[any_space] * 3,
        out_specs=[any_space] * 4,
        scratch_shapes=[
            vm((T, D), BF16), vm((T, D), BF16), vm((D, T), BF16), vm((T, D), BF16), vm((T, D), F32),
            vm((2, D, 2 * HC), BF16), vm((2, HC, D), BF16),
            vm((HC, T), BF16), vm((T, 2 * HC), BF16), vm((2, TT, 2 * HC), F32),
            vm((3, D // 2, HC), F32), vm((3, RD, HC), F32), vm((3, D // 2, HC), BF16), vm((2, 3, D // 2, HC), BF16),
            vm((2, 3, RD // 2, HC), BF16), vm((2, 2, 3, RD // 2, HC), BF16),
            vm((2, 3, RD, HC), BF16), vm((2, 2, 3, RD, HC), BF16), vm((3, RD, HC), BF16),
            pltpu.SemaphoreType.DMA((K, 8)), pltpu.SemaphoreType.DMA((K, 8)),
            pltpu.SemaphoreType.DMA((7,)), pltpu.SemaphoreType.DMA((2, 7)),
            pltpu.SemaphoreType.DMA((2,)), pltpu.SemaphoreType.DMA((2,)),
            pltpu.SemaphoreType.DMA((2,)), pltpu.SemaphoreType.DMA, pltpu.SemaphoreType.DMA((2,)),
        ],
        compiler_params=pltpu.CompilerParams(
            collective_id=0, has_side_effects=True, vmem_limit_bytes=67_000_000
        ),
        cost_estimate=pl.CostEstimate(flops=flops, bytes_accessed=10**8, transcendentals=T * FF),
    )(x, dy, own)


def cut_kernel(wg, wu, wd, own):
    for c in range(NC):
        for i, w in enumerate((wg, wu)):
            parts = [w[0, :, j * (FF // N) + c * SEG : j * (FF // N) + (c + 1) * SEG] for j in range(N)]
            own[c, i] = jnp.concatenate(parts, axis=1)
        for h in range(2):
            own[c, 2, h * SEG : (h + 1) * SEG, :] = wd[0, c * SEG : (c + 1) * SEG, h * HC : (h + 1) * HC]


def cut(wg, wu, wd):
    return pl.pallas_call(
        cut_kernel,
        name="cut",
        grid=(L,),
        out_shape=jax.ShapeDtypeStruct((K, 3, RD, HC), BF16),
        in_specs=[
            pl.BlockSpec((1, RD, FF), lambda n: (n, 0, 0)),
            pl.BlockSpec((1, RD, FF), lambda n: (n, 0, 0)),
            pl.BlockSpec((1, FF // N, D), lambda n: (n, 0, 0)),
        ],
        out_specs=pl.BlockSpec((NC, 3, RD, HC), lambda n: (n, 0, 0, 0)),
    )(wg, wu, wd)


def join_kernel(dx_in, got, dx, wg, wu, wd):
    dx[...] = dx_in[...]
    for i, w in enumerate((wg, wu)):
        parts = [got[c, i, :, j * SEG : (j + 1) * SEG] for j in range(N) for c in range(NC)]
        w[0] = jnp.concatenate(parts, axis=1)
    for c in range(NC):
        for h in range(2):
            wd[0, c * SEG : (c + 1) * SEG, h * HC : (h + 1) * HC] = got[c, 2, h * SEG : (h + 1) * SEG, :]


def join(dx, got):
    return pl.pallas_call(
        join_kernel,
        name="join",
        grid=(L,),
        out_shape=[
            jax.ShapeDtypeStruct((T, D), BF16),
            jax.ShapeDtypeStruct((L, RD, FF), BF16),
            jax.ShapeDtypeStruct((L, RD, FF), BF16),
            jax.ShapeDtypeStruct((L, FF // N, D), BF16),
        ],
        in_specs=[
            pl.BlockSpec((T // L, D), lambda n: (n, 0)),
            pl.BlockSpec((NC, 3, RD, HC), lambda n: (n, 0, 0, 0)),
        ],
        out_specs=[
            pl.BlockSpec((T // L, D), lambda n: (n, 0)),
            pl.BlockSpec((1, RD, FF), lambda n: (n, 0, 0)),
            pl.BlockSpec((1, RD, FF), lambda n: (n, 0, 0)),
            pl.BlockSpec((1, FF // N, D), lambda n: (n, 0, 0)),
        ],
    )(dx, got)


def solution(mesh):
    def body(x, dy, wg, wu, wd):
        dx, got, _, _ = mlp_stack(x[0], dy[0], cut(wg, wu, wd))
        dx, by_g, by_u, by_d = join(dx, got)
        return dx[None], by_g, by_u, by_d

    act = P(("rep", "dp"), None, None)
    w = P(None, "dp", None)
    return jax.shard_map(
        body, mesh=mesh, in_specs=(act, act, w, w, w), out_specs=(act, *[P("rep", "dp", None)] * 3), check_vma=False
    )
```

time: 379 us -> 340 us (0.90)
  local copies, waits for them, and re-layouts: 26.7 us -> 0 us
  Pallas kernels: 349 us -> 340 us
    pallas_call x1, Pallas kernels: 349 us -> 330 us  [mlp_stack(): pl.pallas_call(kernel, name='mlp_stack', out_shape=[jax.ShapeDtypeStruct(...]
    unnamed x9 -> x0, local copies, waits for them, and re-layouts: 11.1 us -> none
    pallas_call x0 -> x2, Pallas kernels: none -> 9.38 us  [the longest x1 5.56 us: join(): pl.pallas_call(join_kernel, name='join', grid=(L,), out_shape=[jax.ShapeD...]
    slice x3 -> x0, local copies, waits for them, and re-layouts: 6.09 us -> none  [the longest x1 3.56 us: body(): out[:, 2].reshape(L, NC, 2, SEG, HC).transpose(0, 1, 3, 2, 4)]
    reshape x3 -> x0, local copies, waits for them, and re-layouts: 5.6 us -> none  [the longest x2 3.82 us: body(): wd.reshape(L, NC, SEG, 2, HC).transpose(0, 1, 3, 2, 4).reshape(K, RD, HC)]
where the time goes in v3:
time: 340 us
  Pallas kernels  340 us (100%)
    pallas_call x1, Pallas kernels, mlp_stack(): pl.pallas_call(kernel, name='mlp_stack', out_shape=[jax.ShapeDtypeStruct(...  330 us

profile of v3, /device:TPU:0, one launch (start us, length us, event | category | flops | bytes accessed | tf_op | source)
XLA Modules:
  0.0 340.2 jit_solution(16216249786887001942)
XLA Ops:
  0.6 3.8 %cut.1.own = bf16[10,3,128,512]{3,2,1,0:T(8,128)(2,1)} custom-call(bf16[2,128,2560]{2,1,0:T(8,128)(2,1)} %wg.1, bf16[2,128,2560]{2,1,0:T(8,128)(2,1)} %wu.1, bf16[2,320,1024]{2,1,0:T(8,128)(2,1)} %wd.1), custom_call_target="tpu_custom_call" | custom-call | tf_op jit(solution)/shard_map/cut/pallas_call | solution.py:426
  4.4 330.1 %mlp_stack.1 = (bf16[2048,1024]{1,0:T(8,128)(2,1)}, bf16[10,3,128,512]{3,2,1,0:T(8,128)(2,1)}, bf16[10,8,3,128,512]{4,3,2,1,0:T(8,128)(2,1)}, f32[20,512,1024]{2,1,0:T(8,128)}) custom-call(bf16[2048,1024]{1,0:T(8,128)(2,1)} %bitcast.3, bf16[2048,1024]{1,0:T(8,128)(2,1)} %bitcast.4, bf16[10,3,128,512]{3,2,1,0:T(8,128)(2,1)} %cut.1.own), custom_call_target="tpu_custom_call" | custom-call | flops 182536110080 | bytes 100000000 | tf_op jit(solution)/shard_map/mlp_stack/pallas_call | solution.py:386
  334.6 5.6 %join.1 = (bf16[2048,1024]{1,0:T(8,128)(2,1)}, bf16[2,128,2560]{2,1,0:T(8,128)(2,1)}, bf16[2,128,2560]{2,1,0:T(8,128)(2,1)}, bf16[2,320,1024]{2,1,0:T(8,128)(2,1)}) custom-call(bf16[2048,1024]{1,0:T(8,128)(2,1)} %get-tuple-element.10.dx_in, bf16[10,3,128,512]{3,2,1,0:T(8,128)(2,1)} %get-tuple-element.11.got), custom_call_target="tpu_custom_call" | custom-call | tf_op jit(solution)/shard_map/join/pallas_call | solution.py:451

commit v4 on v3

--- a/solution.py
+++ b/solution.py
@@ -100,25 +100,17 @@
         pltpu.make_async_copy(wgu.at[slot], wgu.at[slot], gu_sem.at[slot]).wait()
         pltpu.make_async_copy(wdn.at[slot], wdn.at[slot], wd_sem.at[slot]).wait()
 
-    def tick(t):
-        @pl.when(t < K)
-        def _():
-            ag_wait(t, (0, 1))
-            ag_start(t, (3, 4, 5, 6))
-
-        @pl.when(t + 2 < K)
-        def _():
-            ag_start(t + 2, (0, 1, 2))
-
-        @pl.when((t >= 1) & (t - 1 < K))
-        def _():
-            ag_wait(t - 1, (3, 4))
-            ag_start(t - 1, (7,))
-            ag_wait(t - 1, (2, 5, 6, 7))
-
-        @pl.when((t >= 1) & (t - 1 < K + NC))
-        def _():
-            load(t - 1)
+    def begin(k):
+        ag_start(k, (0, 1, 2))
+
+    def forward_on(k):
+        ag_wait(k, (0, 1))
+        ag_start(k, (3, 4, 5, 6))
+
+    def finish(k):
+        ag_wait(k, (3, 4))
+        ag_start(k, (7,))
+        ag_wait(k, (2, 5, 6, 7))
 
     def rs(v, m):
         if m < 3:
@@ -188,7 +180,7 @@
         out_copy(b).start()
 
     def some(i, n):
-        return pl.ds(pl.multiple_of(i * n, n), n)
+        return pl.ds(i * n, n) if isinstance(i, int) else pl.ds(pl.multiple_of(i * n, n), n)
 
     def norm_tile(i):
         rows = some(i, TE)
@@ -219,10 +211,12 @@
     x_copy.start()
     dy_copy.start()
     pl.semaphore_wait(barrier, 3)
-    ag_start(0, (0, 1, 2))
-    ag_start(1, (0, 1, 2))
+    begin(0)
+    begin(1)
     x_copy.wait()
     loop(T // TE, norm_tile)
+    forward_on(0)
+    begin(2)
 
     NT = T // TT
 
@@ -232,32 +226,48 @@
     def reading(g):
         return pltpu.make_async_copy(saved.at[g], gs.at[g % 2], gs_sem.at[g % 2])
 
-    def first(t):
-        tick(t)
-
-        @pl.when(t >= 2)
-        def _():
-            c, slot = t - 2, t % 2
-            load_wait(c)
-
-            def tile(i):
-                g = c * NT + i
-                rows = some(i, TT)
-                both = dot(a_ref[rows, :], wgu[slot])
-
-                @pl.when(g >= 2)
-                def _():
-                    saving(g - 2).wait()
-
-                gs[g % 2] = both
-                saving(g).start()
-                gate, up = both[:, :HC], both[:, HC:]
-                p = (gate * jax.nn.sigmoid(gate) * up).astype(BF16)
-                acc[rows, :] = acc[rows, :] + dot(p, wdn[slot])
-
-            loop(NT, tile)
-
-    loop(NC + 2, first)
+    def first(c):
+        slot = c % 2
+
+        @pl.when(c + 1 < NC)
+        def _():
+            forward_on(c + 1)
+
+        @pl.when(c + 3 < NC)
+        def _():
+            begin(c + 3)
+
+        @pl.when(c == NC - 2)
+        def _():
+            begin(NC)
+
+        finish(c)
+        load(c)
+        load_wait(c)
+
+        def tile(i):
+            @pl.when((c == NC - 1) & (i == NT - 1))
+            def _():
+                forward_on(NC)
+                begin(NC + 1)
+
+            g = c * NT + i
+            rows = some(i, TT)
+            both = dot(a_ref[rows, :], wgu[slot])
+
+            @pl.when(g >= 2)
+            def _():
+                saving(g - 2).wait()
+
+            gs[g % 2] = both
+            saving(g).start()
+            gate, up = both[:, :HC], both[:, HC:]
+            p = (gate * jax.nn.sigmoid(gate) * up).astype(BF16)
+            acc[rows, :] = acc[rows, :] + dot(p, wdn[slot])
+
+        loop(NT, tile)
+
+    loop(NC, first)
 
     def next_state(i):
         rows = some(i, TE)
@@ -270,26 +280,34 @@
     saving(NC * NT - 1).wait()
     reading(0).start()
     reading(1).start()
+    finish(NC)
+    load(NC)
+    begin(NC + 2)
 
     def backward(s, n, tile):
-        tick(s + NC + 2)
         load_wait(s + NC)
         slot = (s + NC) % 2
         v = s % 2
 
-        def step(i):
-            tile(s, i, slot)
-
-            @pl.when((i == 0) & (s >= 1))
-            def _():
-                f2(s - 1)
-
-        loop(n, step)
+        @pl.when(s + NC + 1 < K)
+        def _():
+            forward_on(s + NC + 1)
+
+        loop(n, lambda i: tile(s, i, slot))
+
+        @pl.when(s >= 2)
+        def _():
+            f3(s - 2)
 
         @pl.when(s >= 1)
         def _():
+            f2(s - 1)
             for m in range(3):
                 rs(v, m).wait_send()
+
+        @pl.when(s + NC + 3 < K)
+        def _():
+            begin(s + NC + 3)
 
         top, low = pl.ds(0, D // 2), pl.ds(D // 2, D // 2)
         both = dot(at_ref[low, :], dgu[...])
@@ -311,17 +329,22 @@
                 to = pl.ds(q * RD + h * SEG, SEG)
                 keep[2, to, :] = down[q * SEG : (q + 1) * SEG, h * HC : (h + 1) * HC]
 
-        @pl.when(s >= 1)
-        def _():
-            f3(s - 1)
-
         f1(s)
+
+        @pl.when(s + NC + 1 < K)
+        def _():
+            finish(s + NC + 1)
+
+        @pl.when(s + 1 < K)
+        def _():
+            load(s + NC + 1)
 
         def da_tile(i):
             rows = some(i, TT)
             acc[rows, :] = acc[rows, :] + dot_nt(dgu[rows, :], wgu[slot])
 
-        loop(NT, da_tile)
+        for i in range(NT):
+            da_tile(i)
 
     def hidden(rows, gate, up, slot):
         dp = dot_nt(dh[rows, :], wdn[slot]).astype(BF16).astype(F32)
@@ -362,6 +385,7 @@
     loop(T // TE, norm_tile)
     loop(NC, lambda s: backward(s + NC, NT, read_back))
 
+    f3(K - 2)
     f2(K - 1)
     loop(T // TE, lambda i: norm_back(i, a_ref))
     dx_copy = pltpu.make_async_copy(a_ref, dx_hbm, io_sem.at[1])

time: 340 us -> 331 us (0.974)
  Pallas kernels: 340 us -> 330 us
    pallas_call x1, Pallas kernels: 330 us -> 320 us  [mlp_stack(): pl.pallas_call(kernel, name='mlp_stack', out_shape=[jax.ShapeDtypeStruct(...]
where the time goes in v4:
time: 331 us; the launch traced here: 330 us
  Pallas kernels  330 us (100%)
    pallas_call x1, Pallas kernels, mlp_stack(): pl.pallas_call(kernel, name='mlp_stack', out_shape=[jax.ShapeDtypeStruct(...  320 us

profile of v4, /device:TPU:0, one launch (start us, length us, event | category | flops | bytes accessed | tf_op | source)
XLA Modules:
  0.0 330.3 jit_solution(16298259777517987915)
XLA Ops:
  0.6 3.8 %cut.1.own = bf16[10,3,128,512]{3,2,1,0:T(8,128)(2,1)} custom-call(bf16[2,128,2560]{2,1,0:T(8,128)(2,1)} %wg.1, bf16[2,128,2560]{2,1,0:T(8,128)(2,1)} %wu.1, bf16[2,320,1024]{2,1,0:T(8,128)(2,1)} %wd.1), custom_call_target="tpu_custom_call" | custom-call | tf_op jit(solution)/shard_map/cut/pallas_call | solution.py:450
  4.4 320.2 %mlp_stack.1 = (bf16[2048,1024]{1,0:T(8,128)(2,1)}, bf16[10,3,128,512]{3,2,1,0:T(8,128)(2,1)}, bf16[10,8,3,128,512]{4,3,2,1,0:T(8,128)(2,1)}, f32[20,512,1024]{2,1,0:T(8,128)}) custom-call(bf16[2048,1024]{1,0:T(8,128)(2,1)} %bitcast.3, bf16[2048,1024]{1,0:T(8,128)(2,1)} %bitcast.4, bf16[10,3,128,512]{3,2,1,0:T(8,128)(2,1)} %cut.1.own), custom_call_target="tpu_custom_call" | custom-call | flops 182536110080 | bytes 100000000 | tf_op jit(solution)/shard_map/mlp_stack/pallas_call | solution.py:410
  324.7 5.6 %join.1 = (bf16[2048,1024]{1,0:T(8,128)(2,1)}, bf16[2,128,2560]{2,1,0:T(8,128)(2,1)}, bf16[2,128,2560]{2,1,0:T(8,128)(2,1)}, bf16[2,320,1024]{2,1,0:T(8,128)(2,1)}) custom-call(bf16[2048,1024]{1,0:T(8,128)(2,1)} %get-tuple-element.10.dx_in, bf16[10,3,128,512]{3,2,1,0:T(8,128)(2,1)} %get-tuple-element.11.got), custom_call_target="tpu_custom_call" | custom-call | tf_op jit(solution)/shard_map/join/pallas_call | solution.py:475

commit v5 on v4

--- a/solution.py
+++ b/solution.py
@@ -29,10 +29,10 @@
 
 def kernel(
     x_hbm, dy_hbm, own,
-    dx_hbm, out, land, saved,
+    dx_hbm, out, land, saved, saved_p, saved_a, saved_at,
     xh, a_ref, at_ref, dh, acc, wgu, wdn, pt, dgu, gs,
     keep, mine, send0, recv0, s1, r1, s2, r2, outb,
-    ag_send, ag_recv, rs_send, rs_recv, gu_sem, wd_sem, io_sem, out_sem, gs_sem,
+    ag_send, ag_recv, rs_send, rs_recv, gu_sem, wd_sem, io_sem, out_sem, gs_sem, pt_sem,
 ):
     me = lax.axis_index("dp")
     core = me % 2
@@ -215,17 +215,36 @@
     begin(1)
     x_copy.wait()
     loop(T // TE, norm_tile)
+    a_out = pltpu.make_async_copy(a_ref, saved_a, io_sem.at[2])
+    at_out = pltpu.make_async_copy(at_ref, saved_at, io_sem.at[3])
+    a_out.start()
+    at_out.start()
     forward_on(0)
     begin(2)
 
     NT = T // TT
 
+    def silu(both):
+        gate, up = both[:, :HC], both[:, HC:]
+        sig = jax.nn.sigmoid(gate)
+        act = gate * sig
+        return act, sig + act * (1.0 - sig), up
+
+    def put_p(p, rows):
+        across = p.T
+        for j in range(N):
+            place = ((j % 2 + core) % 2) * (N // 2) + j // 2
+            pt[pl.ds(place * SEG, SEG), rows] = across[j * SEG : (j + 1) * SEG, :]
+
     def saving(g):
         return pltpu.make_async_copy(gs.at[g % 2], saved.at[g], gs_sem.at[g % 2])
 
     def reading(g):
         return pltpu.make_async_copy(saved.at[g], gs.at[g % 2], gs_sem.at[g % 2])
 
+    def keep_p(c):
+        return pltpu.make_async_copy(pt, saved_p.at[c], pt_sem)
+
     def first(c):
         slot = c % 2
 
@@ -241,31 +260,47 @@
         def _():
             begin(NC)
 
-        finish(c)
-        load(c)
+        @pl.when(c < NC - 1)
+        def _():
+            finish(c)
+            load(c)
+
         load_wait(c)
 
         def tile(i):
-            @pl.when((c == NC - 1) & (i == NT - 1))
+            @pl.when((c == NC - 2) & (i == NT - 2))
+            def _():
+                finish(NC - 1)
+                load(NC - 1)
+
+            @pl.when((c == NC - 1) & (i == NT - 2))
             def _():
                 forward_on(NC)
                 begin(NC + 1)
+                begin(NC + 2)
 
             g = c * NT + i
-            rows = some(i, TT)
-            both = dot(a_ref[rows, :], wgu[slot])
 
             @pl.when(g >= 2)
             def _():
                 saving(g - 2).wait()
 
-            gs[g % 2] = both
+            @pl.when((c >= 1) & (i == 0))
+            def _():
+                keep_p(c - 1).wait()
+
+            rows = some(i, TT)
+            both = dot(a_ref[rows, :], wgu[slot])
+            act, slope, up = silu(both)
+            gs[g % 2, :, pl.ds(0, HC)] = act
+            gs[g % 2, :, pl.ds(HC, HC)] = slope * up
             saving(g).start()
-            gate, up = both[:, :HC], both[:, HC:]
-            p = (gate * jax.nn.sigmoid(gate) * up).astype(BF16)
+            p = (act * up).astype(BF16)
+            put_p(p, rows)
             acc[rows, :] = acc[rows, :] + dot(p, wdn[slot])
 
         loop(NT, tile)
+        keep_p(c).start()
 
     loop(NC, first)
 
@@ -274,22 +309,30 @@
         xh[rows, :] = (xh[rows, :].astype(F32) + acc[rows, :].astype(BF16).astype(F32)).astype(BF16)
         norm_tile(i)
 
+    a_out.wait()
+    at_out.wait()
     loop(T // TE, next_state)
     dy_copy.wait()
+    keep_p(NC - 1).wait()
     saving(NC * NT - 2).wait()
     saving(NC * NT - 1).wait()
     reading(0).start()
     reading(1).start()
     finish(NC)
     load(NC)
-    begin(NC + 2)
+
+    def get_p(c):
+        return pltpu.make_async_copy(saved_p.at[c], pt, pt_sem)
+
+    a_in = pltpu.make_async_copy(saved_a, a_ref, io_sem.at[2])
+    at_in = pltpu.make_async_copy(saved_at, at_ref, io_sem.at[3])
 
     def backward(s, n, tile):
         load_wait(s + NC)
         slot = (s + NC) % 2
         v = s % 2
 
-        @pl.when(s + NC + 1 < K)
+        @pl.when((s >= 1) & (s + NC + 1 < K))
         def _():
             forward_on(s + NC + 1)
 
@@ -305,9 +348,17 @@
             for m in range(3):
                 rs(v, m).wait_send()
 
+        @pl.when(s == 0)
+        def _():
+            forward_on(NC + 1)
+
         @pl.when(s + NC + 3 < K)
         def _():
             begin(s + NC + 3)
+
+        @pl.when(s >= NC)
+        def _():
+            get_p(s - NC).wait()
 
         top, low = pl.ds(0, D // 2), pl.ds(D // 2, D // 2)
         both = dot(at_ref[low, :], dgu[...])
@@ -329,6 +380,15 @@
                 to = pl.ds(q * RD + h * SEG, SEG)
                 keep[2, to, :] = down[q * SEG : (q + 1) * SEG, h * HC : (h + 1) * HC]
 
+        @pl.when((s >= NC - 1) & (s + 1 < K))
+        def _():
+            get_p(s + 1 - NC).start()
+
+        @pl.when(s == NC - 1)
+        def _():
+            a_in.start()
+            at_in.start()
+
         f1(s)
 
         @pl.when(s + NC + 1 < K)
@@ -346,45 +406,41 @@
         for i in range(NT):
             da_tile(i)
 
-    def hidden(rows, gate, up, slot):
+    def back_to(rows, act, slope, slot):
         dp = dot_nt(dh[rows, :], wdn[slot]).astype(BF16).astype(F32)
-        sig = jax.nn.sigmoid(gate)
-        act = gate * sig
         dgu[rows, pl.ds(HC, HC)] = (dp * act).astype(BF16)
-        dgu[rows, pl.ds(0, HC)] = (dp * up * (sig + act * (1.0 - sig))).astype(BF16)
-        across = (act * up).astype(BF16).T
-        for j in range(N):
-            place = ((j % 2 + core) % 2) * (N // 2) + j // 2
-            pt[pl.ds(place * SEG, SEG), rows] = across[j * SEG : (j + 1) * SEG, :]
+        dgu[rows, pl.ds(0, HC)] = (dp * slope).astype(BF16)
 
     def computed(s, i, slot):
         rows = some(i, TB)
-        both = dot(a_ref[rows, :], wgu[slot])
-        hidden(rows, both[:, :HC], both[:, HC:], slot)
+        act, slope, up = silu(dot(a_ref[rows, :], wgu[slot]))
+        back_to(rows, act, slope * up, slot)
+        put_p((act * up).astype(BF16), rows)
 
     def read_back(s, i, slot):
         g = (s - NC) * NT + i
         reading(g).wait()
-        hidden(some(i, TT), gs[g % 2, :, pl.ds(0, HC)], gs[g % 2, :, pl.ds(HC, HC)], slot)
+        back_to(some(i, TT), gs[g % 2, :, pl.ds(0, HC)], gs[g % 2, :, pl.ds(HC, HC)], slot)
 
         @pl.when(g + 2 < NC * NT)
         def _():
             reading(g + 2).start()
 
     loop(NC, lambda s: backward(s, T // TB, computed))
-
-    def again(i):
-        return pltpu.make_async_copy(x_hbm.at[some(i, TE)], xh.at[some(i, TE)], io_sem.at[0])
 
     def change(i):
         norm_back(i, dh)
-        again(i).start()
+        rows = some(i, TE)
+        acc[rows, :] = jnp.zeros((TE, D), F32)
 
     loop(T // TE, change)
-    x_copy.wait()
-    loop(T // TE, norm_tile)
+    x_again = pltpu.make_async_copy(x_hbm, xh, io_sem.at[0])
+    x_again.start()
+    a_in.wait()
+    at_in.wait()
     loop(NC, lambda s: backward(s + NC, NT, read_back))
 
+    x_again.wait()
     f3(K - 2)
     f2(K - 1)
     loop(T // TE, lambda i: norm_back(i, a_ref))
@@ -415,9 +471,12 @@
             jax.ShapeDtypeStruct((K, 3, RD, HC), BF16),
             jax.ShapeDtypeStruct((K, N, 3, RD, HC), BF16),
             jax.ShapeDtypeStruct((NC * (T // TT), TT, 2 * HC), F32),
+            jax.ShapeDtypeStruct((NC, HC, T), BF16),
+            jax.ShapeDtypeStruct((T, D), BF16),
+            jax.ShapeDtypeStruct((D, T), BF16),
         ],
         in_specs=[any_space] * 3,
-        out_specs=[any_space] * 4,
+        out_specs=[any_space] * 7,
         scratch_shapes=[
             vm((T, D), BF16), vm((T, D), BF16), vm((D, T), BF16), vm((T, D), BF16), vm((T, D), F32),
             vm((2, D, 2 * HC), BF16), vm((2, HC, D), BF16),
@@ -428,7 +487,7 @@
             pltpu.SemaphoreType.DMA((K, 8)), pltpu.SemaphoreType.DMA((K, 8)),
             pltpu.SemaphoreType.DMA((7,)), pltpu.SemaphoreType.DMA((2, 7)),
             pltpu.SemaphoreType.DMA((2,)), pltpu.SemaphoreType.DMA((2,)),
-            pltpu.SemaphoreType.DMA((2,)), pltpu.SemaphoreType.DMA, pltpu.SemaphoreType.DMA((2,)),
+            pltpu.SemaphoreType.DMA((4,)), pltpu.SemaphoreType.DMA, pltpu.SemaphoreType.DMA((2,)), pltpu.SemaphoreType.DMA,
         ],
         compiler_params=pltpu.CompilerParams(
             collective_id=0, has_side_effects=True, vmem_limit_bytes=67_000_000
@@ -497,7 +556,7 @@
 
 def solution(mesh):
     def body(x, dy, wg, wu, wd):
-        dx, got, _, _ = mlp_stack(x[0], dy[0], cut(wg, wu, wd))
+        dx, got, *_ = mlp_stack(x[0], dy[0], cut(wg, wu, wd))
         dx, by_g, by_u, by_d = join(dx, got)
         return dx[None], by_g, by_u, by_d
 

time: 331 us -> 319 us (0.964)
  Pallas kernels: 330 us -> 318 us
    pallas_call x1, Pallas kernels: 320 us -> 308 us  [mlp_stack(): pl.pallas_call(kernel, name='mlp_stack', out_shape=[jax.ShapeDtypeStruct(...]
where the time goes in v5:
time: 319 us; the launch traced here: 318 us
  Pallas kernels  318 us (100%)
    pallas_call x1, Pallas kernels, mlp_stack(): pl.pallas_call(kernel, name='mlp_stack', out_shape=[jax.ShapeDtypeStruct(...  308 us

profile of v5, /device:TPU:0, one launch (start us, length us, event | category | flops | bytes accessed | tf_op | source)
XLA Modules:
  0.0 318.3 jit_solution(14528361339083612966)
XLA Ops:
  0.6 3.8 %cut.1.own = bf16[10,3,128,512]{3,2,1,0:T(8,128)(2,1)} custom-call(bf16[2,128,2560]{2,1,0:T(8,128)(2,1)} %wg.1, bf16[2,128,2560]{2,1,0:T(8,128)(2,1)} %wu.1, bf16[2,320,1024]{2,1,0:T(8,128)(2,1)} %wd.1), custom_call_target="tpu_custom_call" | custom-call | tf_op jit(solution)/shard_map/cut/pallas_call | solution.py:509
  4.4 308.3 %mlp_stack.1 = (bf16[2048,1024]{1,0:T(8,128)(2,1)}, bf16[10,3,128,512]{3,2,1,0:T(8,128)(2,1)}, bf16[10,8,3,128,512]{4,3,2,1,0:T(8,128)(2,1)}, f32[20,512,1024]{2...) custom-call(bf16[2048,1024]{1,0:T(8,128)(2,1)} %bitcast.3, ...), custom_call_target="tpu_custom_call" | custom-call | flops 182536110080 | bytes 100000000 | tf_op jit(solution)/shard_map/mlp_stack/pallas_call | solution.py:466
  312.7 5.6 %join.1 = (bf16[2048,1024]{1,0:T(8,128)(2,1)}, bf16[2,128,2560]{2,1,0:T(8,128)(2,1)}, bf16[2,128,2560]{2,1,0:T(8,128)(2,1)}, bf16[2,320,1024]{2,1,0:T(8,128)(2,1)}) custom-call(bf16[2048,1024]{1,0:T(8,128)(2,1)} %get-tuple-element.10.dx_in, bf16[10,3,128,512]{3,2,1,0:T(8,128)(2,1)} %get-tuple-element.11.got), custom_call_target="tpu_custom_call" | custom-call | tf_op jit(solution)/shard_map/join/pallas_call | solution.py:534

commit v6 on v5

--- a/solution.py
+++ b/solution.py
@@ -29,11 +29,12 @@
 
 def kernel(
     x_hbm, dy_hbm, own,
-    dx_hbm, out, land, saved, saved_p, saved_a, saved_at,
-    xh, a_ref, at_ref, dh, acc, wgu, wdn, pt, dgu, gs,
+    dx_hbm, out, land, saved, saved_p, saved_at,
+    xh, two, at_ref, dh, acc, wgu, wdn, pt, gs,
     keep, mine, send0, recv0, s1, r1, s2, r2, outb,
     ag_send, ag_recv, rs_send, rs_recv, gu_sem, wd_sem, io_sem, out_sem, gs_sem, pt_sem,
 ):
+    a_ref, dgu = two.at[0], two.at[1]
     me = lax.axis_index("dp")
     core = me % 2
     ypos = (me // 2) % 2
@@ -215,9 +216,7 @@
     begin(1)
     x_copy.wait()
     loop(T // TE, norm_tile)
-    a_out = pltpu.make_async_copy(a_ref, saved_a, io_sem.at[2])
     at_out = pltpu.make_async_copy(at_ref, saved_at, io_sem.at[3])
-    a_out.start()
     at_out.start()
     forward_on(0)
     begin(2)
@@ -273,7 +272,7 @@
                 finish(NC - 1)
                 load(NC - 1)
 
-            @pl.when((c == NC - 1) & (i == NT - 2))
+            @pl.when((c == NC - 1) & (i == 1))
             def _():
                 forward_on(NC)
                 begin(NC + 1)
@@ -305,11 +304,15 @@
     loop(NC, first)
 
     def next_state(i):
+        @pl.when(i == T // TE - 3)
+        def _():
+            finish(NC)
+            load(NC)
+
         rows = some(i, TE)
         xh[rows, :] = (xh[rows, :].astype(F32) + acc[rows, :].astype(BF16).astype(F32)).astype(BF16)
         norm_tile(i)
 
-    a_out.wait()
     at_out.wait()
     loop(T // TE, next_state)
     dy_copy.wait()
@@ -318,16 +321,19 @@
     saving(NC * NT - 1).wait()
     reading(0).start()
     reading(1).start()
-    finish(NC)
-    load(NC)
 
     def get_p(c):
         return pltpu.make_async_copy(saved_p.at[c], pt, pt_sem)
 
-    a_in = pltpu.make_async_copy(saved_a, a_ref, io_sem.at[2])
     at_in = pltpu.make_async_copy(saved_at, at_ref, io_sem.at[3])
 
-    def backward(s, n, tile):
+    def add_da(s, buf):
+        slot = (s + NC) % 2
+        for i in range(NT):
+            rows = some(i, TT)
+            acc[rows, :] = acc[rows, :] + dot_nt(buf[rows, :], wgu[slot])
+
+    def backward(s, n, tile, buf, da=None):
         load_wait(s + NC)
         slot = (s + NC) % 2
         v = s % 2
@@ -336,7 +342,7 @@
         def _():
             forward_on(s + NC + 1)
 
-        loop(n, lambda i: tile(s, i, slot))
+        loop(n, lambda i: tile(s, i, slot, buf))
 
         @pl.when(s >= 2)
         def _():
@@ -361,7 +367,7 @@
             get_p(s - NC).wait()
 
         top, low = pl.ds(0, D // 2), pl.ds(D // 2, D // 2)
-        both = dot(at_ref[low, :], dgu[...])
+        both = dot(at_ref[low, :], buf[...])
         for i in range(2):
             send0[i] = both[:, i * HC : (i + 1) * HC].astype(BF16)
             rs(v, i).start()
@@ -371,7 +377,7 @@
                 to = pl.ds(q * RD + h * SEG, SEG)
                 send0[2, to, :] = down[q * SEG : (q + 1) * SEG, h * HC : (h + 1) * HC].astype(BF16)
         rs(v, 2).start()
-        both = dot(at_ref[top, :], dgu[...])
+        both = dot(at_ref[top, :], buf[...])
         for i in range(2):
             keep[i] = both[:, i * HC : (i + 1) * HC]
         down = dot(pt[pl.ds(0, HC // 2), :], dh[...])
@@ -386,7 +392,6 @@
 
         @pl.when(s == NC - 1)
         def _():
-            a_in.start()
             at_in.start()
 
         f1(s)
@@ -399,34 +404,30 @@
         def _():
             load(s + NC + 1)
 
-        def da_tile(i):
-            rows = some(i, TT)
-            acc[rows, :] = acc[rows, :] + dot_nt(dgu[rows, :], wgu[slot])
-
-        for i in range(NT):
-            da_tile(i)
-
-    def back_to(rows, act, slope, slot):
+        if da is not None:
+            pl.when(da(s))(lambda: add_da(s, buf))
+
+    def back_to(rows, act, slope, slot, buf):
         dp = dot_nt(dh[rows, :], wdn[slot]).astype(BF16).astype(F32)
-        dgu[rows, pl.ds(HC, HC)] = (dp * act).astype(BF16)
-        dgu[rows, pl.ds(0, HC)] = (dp * slope).astype(BF16)
-
-    def computed(s, i, slot):
+        buf[rows, pl.ds(HC, HC)] = (dp * act).astype(BF16)
+        buf[rows, pl.ds(0, HC)] = (dp * slope).astype(BF16)
+
+    def computed(s, i, slot, buf):
         rows = some(i, TB)
         act, slope, up = silu(dot(a_ref[rows, :], wgu[slot]))
-        back_to(rows, act, slope * up, slot)
+        back_to(rows, act, slope * up, slot, buf)
         put_p((act * up).astype(BF16), rows)
 
-    def read_back(s, i, slot):
+    def read_back(s, i, slot, buf):
         g = (s - NC) * NT + i
         reading(g).wait()
-        back_to(some(i, TT), gs[g % 2, :, pl.ds(0, HC)], gs[g % 2, :, pl.ds(HC, HC)], slot)
+        back_to(some(i, TT), gs[g % 2, :, pl.ds(0, HC)], gs[g % 2, :, pl.ds(HC, HC)], slot, buf)
 
         @pl.when(g + 2 < NC * NT)
         def _():
             reading(g + 2).start()
 
-    loop(NC, lambda s: backward(s, T // TB, computed))
+    loop(NC, lambda s: backward(s, T // TB, computed, dgu, lambda s: s >= 0))
 
     def change(i):
         norm_back(i, dh)
@@ -436,13 +437,23 @@
     loop(T // TE, change)
     x_again = pltpu.make_async_copy(x_hbm, xh, io_sem.at[0])
     x_again.start()
-    a_in.wait()
     at_in.wait()
-    loop(NC, lambda s: backward(s + NC, NT, read_back))
-
-    x_again.wait()
-    f3(K - 2)
-    f2(K - 1)
+
+    def last_layer(s):
+        backward(s, NT, read_back, two.at[1 - s // (K - 1)], lambda s: s < K - 2)
+
+    loop(NC, lambda s: last_layer(s + NC))
+
+    def late_da(j):
+        @pl.when(j == 1)
+        def _():
+            x_again.wait()
+            f3(K - 2)
+            f2(K - 1)
+
+        add_da(K - 2 + j, two.at[1 - j])
+
+    loop(2, late_da)
     loop(T // TE, lambda i: norm_back(i, a_ref))
     dx_copy = pltpu.make_async_copy(a_ref, dx_hbm, io_sem.at[1])
     dx_copy.start()
@@ -472,15 +483,14 @@
             jax.ShapeDtypeStruct((K, N, 3, RD, HC), BF16),
             jax.ShapeDtypeStruct((NC * (T // TT), TT, 2 * HC), F32),
             jax.ShapeDtypeStruct((NC, HC, T), BF16),
-            jax.ShapeDtypeStruct((T, D), BF16),
             jax.ShapeDtypeStruct((D, T), BF16),
         ],
         in_specs=[any_space] * 3,
-        out_specs=[any_space] * 7,
+        out_specs=[any_space] * 6,
         scratch_shapes=[
-            vm((T, D), BF16), vm((T, D), BF16), vm((D, T), BF16), vm((T, D), BF16), vm((T, D), F32),
+            vm((T, D), BF16), vm((2, T, D), BF16), vm((D, T), BF16), vm((T, D), BF16), vm((T, D), F32),
             vm((2, D, 2 * HC), BF16), vm((2, HC, D), BF16),
-            vm((HC, T), BF16), vm((T, 2 * HC), BF16), vm((2, TT, 2 * HC), F32),
+            vm((HC, T), BF16), vm((2, TT, 2 * HC), F32),
             vm((3, D // 2, HC), F32), vm((3, RD, HC), F32), vm((3, D // 2, HC), BF16), vm((2, 3, D // 2, HC), BF16),
             vm((2, 3, RD // 2, HC), BF16), vm((2, 2, 3, RD // 2, HC), BF16),
             vm((2, 3, RD, HC), BF16), vm((2, 2, 3, RD, HC), BF16), vm((3, RD, HC), BF16),

time: 319 us -> 315 us (0.987)
  Pallas kernels: 318 us -> 314 us
    pallas_call x1, Pallas kernels: 308 us -> 305 us  [mlp_stack(): pl.pallas_call(kernel, name='mlp_stack', out_shape=[jax.ShapeDtypeStruct(...]
where the time goes in v6:
time: 315 us
  Pallas kernels  314 us (100%)
    pallas_call x1, Pallas kernels, mlp_stack(): pl.pallas_call(kernel, name='mlp_stack', out_shape=[jax.ShapeDtypeStruct(...  305 us

profile of v6, /device:TPU:0, one launch (start us, length us, event | category | flops | bytes accessed | tf_op | source)
XLA Modules:
  0.0 315.1 jit_solution(2443655571151529671)
XLA Ops:
  0.6 3.8 %cut.1.own = bf16[10,3,128,512]{3,2,1,0:T(8,128)(2,1)} custom-call(bf16[2,128,2560]{2,1,0:T(8,128)(2,1)} %wg.1, bf16[2,128,2560]{2,1,0:T(8,128)(2,1)} %wu.1, bf16[2,320,1024]{2,1,0:T(8,128)(2,1)} %wd.1), custom_call_target="tpu_custom_call" | custom-call | tf_op jit(solution)/shard_map/cut/pallas_call | solution.py:519
  4.4 305.1 %mlp_stack.1 = (bf16[2048,1024]{1,0:T(8,128)(2,1)}, bf16[10,3,128,512]{3,2,1,0:T(8,128)(2,1)}, bf16[10,8,3,128,512]{4,3,2,1,0:T(8,128)(2,1)}, f32[20,512,1024]{2...) custom-call(bf16[2048,1024]{1,0:T(8,128)(2,1)} %bitcast.3, bf16[2048,1024]{1,0:T(8,128)(2,1)} %bitcast.4, ...), custom_call_target="tpu_custom_call" | custom-call | flops 182536110080 | bytes 100000000 | tf_op jit(solution)/shard_map/mlp_stack/pallas_call | solution.py:477
  309.5 5.6 %join.1 = (bf16[2048,1024]{1,0:T(8,128)(2,1)}, bf16[2,128,2560]{2,1,0:T(8,128)(2,1)}, bf16[2,128,2560]{2,1,0:T(8,128)(2,1)}, bf16[2,320,1024]{2,1,0:T(8,128)(2,1)}) custom-call(bf16[2048,1024]{1,0:T(8,128)(2,1)} %get-tuple-element.10.dx_in, bf16[10,3,128,512]{3,2,1,0:T(8,128)(2,1)} %get-tuple-element.11.got), custom_call_target="tpu_custom_call" | custom-call | tf_op jit(solution)/shard_map/join/pallas_call | solution.py:544

commit v7 on v6

--- a/solution.py
+++ b/solution.py
@@ -357,10 +357,6 @@
         @pl.when(s == 0)
         def _():
             forward_on(NC + 1)
-
-        @pl.when(s + NC + 3 < K)
-        def _():
-            begin(s + NC + 3)
 
         @pl.when(s >= NC)
         def _():
@@ -395,6 +391,10 @@
             at_in.start()
 
         f1(s)
+
+        @pl.when(s + NC + 3 < K)
+        def _():
+            begin(s + NC + 3)
 
         @pl.when(s + NC + 1 < K)
         def _():

time: 315 us -> 314 us (level)
  no operation moved by 1% of the time
where the time goes in v7:
time: 314 us
  Pallas kernels  313 us (100%)
    pallas_call x1, Pallas kernels, mlp_stack(): pl.pallas_call(kernel, name='mlp_stack', out_shape=[jax.ShapeDtypeStruct(...  304 us

profile of v7, /device:TPU:0, one launch (start us, length us, event | category | flops | bytes accessed | tf_op | source)
XLA Modules:
  0.0 313.7 jit_solution(12138989663154111815)
XLA Ops:
  0.6 3.8 %cut.1.own = bf16[10,3,128,512]{3,2,1,0:T(8,128)(2,1)} custom-call(bf16[2,128,2560]{2,1,0:T(8,128)(2,1)} %wg.1, bf16[2,128,2560]{2,1,0:T(8,128)(2,1)} %wu.1, bf16[2,320,1024]{2,1,0:T(8,128)(2,1)} %wd.1), custom_call_target="tpu_custom_call" | custom-call | tf_op jit(solution)/shard_map/cut/pallas_call | solution.py:519
  4.4 303.7 %mlp_stack.1 = (bf16[2048,1024]{1,0:T(8,128)(2,1)}, bf16[10,3,128,512]{3,2,1,0:T(8,128)(2,1)}, bf16[10,8,3,128,512]{4,3,2,1,0:T(8,128)(2,1)}, f32[20,512,1024]{2...) custom-call(bf16[2048,1024]{1,0:T(8,128)(2,1)} %bitcast.3, bf16[2048,1024]{1,0:T(8,128)(2,1)} %bitcast.4, ...), custom_call_target="tpu_custom_call" | custom-call | flops 182536110080 | bytes 100000000 | tf_op jit(solution)/shard_map/mlp_stack/pallas_call | solution.py:477
  308.2 5.6 %join.1 = (bf16[2048,1024]{1,0:T(8,128)(2,1)}, bf16[2,128,2560]{2,1,0:T(8,128)(2,1)}, bf16[2,128,2560]{2,1,0:T(8,128)(2,1)}, bf16[2,320,1024]{2,1,0:T(8,128)(2,1)}) custom-call(bf16[2048,1024]{1,0:T(8,128)(2,1)} %get-tuple-element.10.dx_in, bf16[10,3,128,512]{3,2,1,0:T(8,128)(2,1)} %get-tuple-element.11.got), custom_call_target="tpu_custom_call" | custom-call | tf_op jit(solution)/shard_map/join/pallas_call | solution.py:544
